TPU v7x, 32 devices: a whole 2x2x4 slice. The times are simulated.
32 devices in a mesh: px: 4 (over y, x), py: 8 (over z, core).
Axes of the slice: x: 2, y: 2, z: 4, core: 2. Of those that a mesh axis runs over, the one named last changes fastest.
Arguments:
- coefficients: bfloat16 [384, 12288], P(('px', 'py')), may hold values from -6 to 6
- exponents: int32 [96, 768], P(('px', 'py')), may hold values from -4 to 1
- right_side: float32 [64, 192, 384], P('px', 'py'), may hold values from -18 to 18
Outputs:
- decoded: float32 [64, 192, 384], P('px', 'py')
- residual: float32 [64, 192, 384], P('px', 'py')
- rms: float32 [], replicated
All inputs are finite; a program needn't handle non-finite values.
Results may differ from a plain program's by a relative error of at most 0.0003.
Values may be sent and summed in bfloat16 or wider, within the bound.
No kernel may reach another device: no remote copies, remote signals or barrier semaphores. Data moves between devices by JAX's collectives and lax.ppermute only.
A program may use at most 64 MiB of HBM per device.

v0:
```python
import jax
import jax.numpy as jnp
from jax import lax
from jax.sharding import PartitionSpec as P

CX = 16
CY = 24


def with_halo(cells, sides, width):
    for axis, dim in sides:
        count = lax.axis_size(axis)
        ends = count - 1
        head = lax.slice_in_dim(cells, 0, width, axis=dim)
        tail = lax.slice_in_dim(cells, cells.shape[dim] - width, cells.shape[dim], axis=dim)
        cells = jnp.concatenate(
            [
                lax.ppermute(tail, axis, [(i, (i + 1) % count) for i in range(ends)]),
                cells,
                lax.ppermute(head, axis, [((i + 1) % count, i) for i in range(ends)]),
            ],
            axis=dim,
        )
    return cells


def block_basis(width):
    rows = jnp.arange(width, dtype=jnp.int32)[:, None]
    cols = jnp.arange(width, dtype=jnp.int32)[None, :]
    frequency = (rows % 4).astype(jnp.float32)
    point = (cols % 4).astype(jnp.float32)
    weight = jnp.where(frequency == 0, jnp.sqrt(jnp.float32(0.25)), jnp.sqrt(jnp.float32(0.5)))
    entry = weight * jnp.cos(jnp.pi * (2.0 * point + 1.0) * frequency / 8.0)
    return jnp.where(rows // 4 == cols // 4, entry, 0.0)


def plane_table():
    across_x = block_basis(CX)
    across_y = block_basis(CY)
    return jnp.einsum("ux,vy->uvxy", across_x, across_y).reshape(CX * CY, CX * CY)


def spread_table():
    quarter_y = CY // 4
    blocks = jnp.arange(CX // 4 * quarter_y, dtype=jnp.int32)[:, None]
    cells = jnp.arange(CX * CY, dtype=jnp.int32)[None, :]
    same_x = cells // CY // 4 == blocks // quarter_y
    same_y = cells % CY // 4 == blocks % quarter_y
    return jnp.where(same_x & same_y, 1.0, 0.0).astype(jnp.float32)


def apply_plane(layers, table):
    return jnp.einsum(
        "zpc,cv->zpv", layers.astype(jnp.float32), table, precision=lax.Precision.HIGHEST
    )


def shards(coefficients, exponents, right_side):
    count_x = lax.axis_size("px")
    count_y = lax.axis_size("py")
    peers = count_x * count_y
    patch = CX * CY
    layer_count = coefficients.shape[0]
    block_layers = exponents.shape[0]
    table = plane_table()
    factor = jnp.exp2(exponents.astype(jnp.float32)).reshape(block_layers, peers, -1)
    spread = jnp.einsum("zpq,qc->zpc", factor, spread_table(), precision=lax.Precision.HIGHEST)
    spread = jnp.broadcast_to(spread[:, None], (block_layers, 4, peers, patch)).reshape(
        layer_count, peers, patch
    )
    scaled = (coefficients.astype(jnp.float32).reshape(layer_count, peers, patch) * spread).astype(
        jnp.bfloat16
    )
    received = lax.all_to_all(scaled, ("px", "py"), split_axis=1, concat_axis=1, tiled=True)
    arrived = apply_plane(received, table)
    stacked = arrived.transpose(1, 0, 2).reshape(-1, 128, patch)
    depth_table = block_basis(128)
    decoded = jnp.einsum(
        "nzq,zw->qnw", stacked, depth_table, precision=lax.Precision.HIGHEST
    ).reshape(CX, CY, -1)
    padded = with_halo(decoded, (("px", 0), ("py", 1)), 1)
    padded = jnp.pad(padded, ((0, 0), (0, 0), (1, 1)))
    beside = padded[2:, 1:-1, 1:-1] + padded[:-2, 1:-1, 1:-1]
    beside = beside + padded[1:-1, 2:, 1:-1] + padded[1:-1, :-2, 1:-1]
    beside = beside + padded[1:-1, 1:-1, 2:] + padded[1:-1, 1:-1, :-2]
    residual = right_side - (6.0 * decoded - beside)
    local_sum = jnp.sum(residual * residual)
    total_sum = lax.psum(local_sum, ("px", "py"))
    cell_count = decoded.shape[0] * decoded.shape[1] * decoded.shape[2] * count_x * count_y
    rms = jnp.sqrt(total_sum / cell_count + 1e-06)
    return (decoded, residual, rms)


def solution(mesh):
    return jax.shard_map(
        shards,
        mesh=mesh,
        in_specs=(P(("px", "py"), None), P(("px", "py"), None), P("px", "py", None)),
        out_specs=(P("px", "py", None), P("px", "py", None), P()),
        check_vma=False,
    )
```

profile of v0, /device:TPU:0, one launch (start us, length us, event | category | flops | bytes accessed | tf_op | source)
XLA Modules:
  0.0 87.5 jit_solution(5199137240304117079)
XLA Ops:
  0.7 0.7 multiply_exponential_fusion
  1.4 0.1 reshape.520
  1.5 1.1 %reshape.525 = f32[12,12288]{1,0:T(8,128)S(1)} convert(bf16[12,12288]{1,0:T(8,128)(2,1)} %param.3) | non-fusion elementwise | flops 147456 | bytes 884736 | tf_op jit(solution)/shard_map/reshape | solution.py:71
  2.5 0.2 copy.34
  2.7 0.3 fusion.15
  3.0 0.1 fusion.1
  3.1 0.8 copy.27
  3.9 7.3 %all-to-all-start = ((bf16[12,32,384]{2,0,1:T(8,128)(2,1)}), bf16[12,32,384]{2,0,1:T(8,128)(2,1)S(1)}, u32[]{:S(2)}, u32[]{:S(2)}) async-start(bf16[12,32,384]{2,0,1:T(8,128)(2,1)} %copy.27), calls=%async_computation | async-start | bytes 786432 | tf_op jit(solution)/shard_map/all_to_all | solution.py:74
  11.3 0.1 multiply_select_fusion
  11.5 0.1 multiply_select_fusion.1
  11.6 0.3 multiply_bitcast_fusion
  11.9 2.3 %reshape.528 = f32[384,384,1]{1,0,2:T(8,128)} reshape(f32[16,24,16,24]{3,2,1,0:T(8,128)S(1)} %multiply_bitcast_fusion) | data formatting | bytes 1179648 | tf_op jit(solution)/shard_map/reshape | solution.py:40
  14.3 10.4 %all-to-all-done = bf16[12,32,384]{2,0,1:T(8,128)(2,1)S(1)} async-done(((bf16[12,32,384]{2,0,1:T(8,128)(2,1)}), bf16[12,32,384]{2,0,1:T(8,128)(2,1)S(1)}, u32[]{:S(2)}, u32[]{:S(2)}) %all-to-all-start) | async-done | bytes 294944 | tf_op jit(solution)/shard_map/all_to_all | solution.py:74
  24.7 1.8 %convolution_bitcast_fusion.1 = f32[32,12,384]{2,0,1:T(8,128)S(1)} fusion(f32[384,384,1]{1,0,2:T(8,128)} %reshape.528, bf16[12,32,384]{2,0,1:T(8,128)(2,1)S(1)} %all-to-all-done), kind=kOutput, calls=%fused_computation.4 | convolution fusion | flops 679477248 | bytes 1474560 | tf_op jit(solution)/shard_map/zpc,cv->zpv/dot_general | solution.py:53
  26.5 0.4 copy.29
  26.9 0.1 reshape.523
  27.0 0.9 %convolution_bitcast_fusion = f32[384,3,128]{0,2,1:T(8,128)S(1)} fusion(f32[3,128,384]{2,1,0:T(8,128)S(1)} %reshape.523, f32[128]{0:T(128)S(1)} %get-tuple-element.27, f32[128]{0:T(128)S(1)} %get-tuple-element.25, f32[128]{0:T(128)S(1)} %get-tuple-element.24, s32[128]{0:T(128)S(1)} %get-tuple-element.26), kind=kOutput, calls=%fused_computation.3 | convolution fusion | flops 226574336 | bytes 1181696 | tf_op jit(solution)/shard_map/nzq,zw->qnw/dot_general | solution.py:78
  27.9 0.1 fusion.54
  28.0 0.1 copy.32
  28.1 1.5 %collective-permute-start.1 = (f32[1,24,384]{2,1,0:T(8,128)S(1)}, f32[1,24,384]{2,1,0:T(8,128)S(1)}, u32[]{:S(2)}, u32[]{:S(2)}) collective-permute-start(f32[1,24,384]{2,1,0:T(8,128)S(1)} %copy.32), channel_id=1, source_target_pairs={{0,8},{8,16},{16,24},{1,9},{9,17},{17,25},{2,10},{10,18},{18,26},{... | collective-permute-start | bytes 110600 | tf_op jit(solution)/shard_map/ppermute | solution.py:18
  29.6 0.3 copy.30
  29.9 0.3 reshape.524
  30.3 0.0 copy-start
  30.3 0.1 copy.31
  30.4 1.3 %collective-permute-start = (f32[1,24,384]{2,1,0:T(8,128)S(1)}, f32[1,24,384]{2,1,0:T(8,128)S(1)}, u32[]{:S(2)}, u32[]{:S(2)}) collective-permute-start(f32[1,24,384]{2,1,0:T(8,128)S(1)} %copy.31), channel_id=1, source_target_pairs={{8,0},{16,8},{24,16},{9,1},{17,9},{25,17},{10,2},{18,10},{26,18},{... | collective-permute-start | bytes 110600 | tf_op jit(solution)/shard_map/ppermute | solution.py:20
  31.7 0.0 collective-permute-done.1
  31.7 0.0 copy-start.1
  31.8 4.9 %collective-permute-done = f32[1,24,384]{2,1,0:T(8,128)S(1)} collective-permute-done((f32[1,24,384]{2,1,0:T(8,128)S(1)}, f32[1,24,384]{2,1,0:T(8,128)S(1)}, u32[]{:S(2)}, u32[]{:S(2)}) %collective-permute-start) | collective-permute-done | bytes 36896 | tf_op jit(solution)/shard_map/ppermute | solution.py:20
  36.8 1.3 %collective-permute-start.2 = (f32[18,1,384]{2,1,0:T(1,128)S(1)}, f32[18,1,384]{2,1,0:T(1,128)S(1)}, u32[]{:S(2)}, u32[]{:S(2)}) collective-permute-start(f32[18,1,384]{2,1,0:T(1,128)S(1)} %get-tuple-element.9), channel_id=1, source_target_pairs={{1,0},{2,1},{3,2},{4,3},{5,4},{6,5},{7,6},{9,8},{10,9},{11,10},{12... | collective-permute-start | bytes 82952 | tf_op jit(solution)/shard_map/ppermute | solution.py:20
  38.1 3.0 %collective-permute-start.3 = (f32[18,1,384]{2,1,0:T(1,128)S(1)}, f32[18,1,384]{2,1,0:T(1,128)S(1)}, u32[]{:S(2)}, u32[]{:S(2)}) collective-permute-start(f32[18,1,384]{2,1,0:T(1,128)S(1)} %get-tuple-element.8), channel_id=1, source_target_pairs={{0,1},{1,2},{2,3},{3,4},{4,5},{5,6},{6,7},{8,9},{9,10},{10,11},{11... | collective-permute-start | bytes 82952 | tf_op jit(solution)/shard_map/ppermute | solution.py:18
  41.1 0.0 collective-permute-done.2
  41.1 0.8 collective-permute-done.3
  41.9 0.6 select_maximum_fusion
  42.5 0.0 copy-done
  42.5 0.0 copy-done.1
  42.5 1.9 %multiply_reduce_fusion = (f32[]{:T(128)}, f32[16,24,384]{2,1,0:T(8,128)}) fusion(f32[16,24,384]{2,1,0:T(8,128)S(1)} %copy-done.1, f32[18,26,386]{2,1,0:T(8,128)S(1)} %select_maximum_fusion, f32[18,24,384]{2,1,0:T(8,128)S(1)} %constant_dynamic-update-slice_fusion, f32[18,1,384]{2,1,0:T(1,128)S(1)} %collective-permute-done.3, ...), kind=kLoop, calls=%fused_computation.21 | loop fusion | flops 2064383 | bytes 3741700 | tf_op jit(solution)/shard_map/reduce_sum | solution.py:87
  44.4 41.2 %psum.7 = f32[]{:T(128)} all-reduce(f32[]{:T(128)} %get-tuple-element.6), channel_id=1, replica_groups=mesh['px'=4,'py'=8] {'px','py'}, use_global_device_ids=true, to_apply=%region_1.2 | all-reduce | flops 1 | bytes 8 | tf_op jit(solution)/shard_map/psum | solution.py:88
  (12 shorter events, 0.2 us)
Async XLA Ops:
  3.9 20.8 %all-to-all-start = ((bf16[12,32,384]{2,0,1:T(8,128)(2,1)}), bf16[12,32,384]{2,0,1:T(8,128)(2,1)S(1)}, u32[]{:S(2)}, u32[]{:S(2)}) async-start(bf16[12,32,384]{2,0,1:T(8,128)(2,1)} %copy.27), calls=%async_computation | async-start | bytes 786432 | tf_op jit(solution)/shard_map/all_to_all | solution.py:74
  28.1 3.6 %collective-permute-start.1 = (f32[1,24,384]{2,1,0:T(8,128)S(1)}, f32[1,24,384]{2,1,0:T(8,128)S(1)}, u32[]{:S(2)}, u32[]{:S(2)}) collective-permute-start(f32[1,24,384]{2,1,0:T(8,128)S(1)} %copy.32), channel_id=1, source_target_pairs={{0,8},{8,16},{16,24},{1,9},{9,17},{17,25},{2,10},{10,18},{18,26},{... | collective-permute-start | bytes 110600 | tf_op jit(solution)/shard_map/ppermute | solution.py:18
  30.3 12.3 %copy-start = (f32[16,24,384]{2,1,0:T(8,128)}, f32[16,24,384]{2,1,0:T(8,128)S(1)}, u32[]{:S(2)}) copy-start(f32[16,24,384]{2,1,0:T(8,128)S(1)} %reshape.524) | copy-start | bytes 1769476
  30.4 6.3 %collective-permute-start = (f32[1,24,384]{2,1,0:T(8,128)S(1)}, f32[1,24,384]{2,1,0:T(8,128)S(1)}, u32[]{:S(2)}, u32[]{:S(2)}) collective-permute-start(f32[1,24,384]{2,1,0:T(8,128)S(1)} %copy.31), channel_id=1, source_target_pairs={{8,0},{16,8},{24,16},{9,1},{17,9},{25,17},{10,2},{18,10},{26,18},{... | collective-permute-start | bytes 110600 | tf_op jit(solution)/shard_map/ppermute | solution.py:20
  31.7 10.8 %copy-start.1 = (f32[16,24,384]{2,1,0:T(8,128)S(1)}, f32[16,24,384]{2,1,0:T(8,128)}, u32[]{:S(2)}) copy-start(f32[16,24,384]{2,1,0:T(8,128)} %param.5) | copy-start | bytes 1769476
  36.8 4.3 %collective-permute-start.2 = (f32[18,1,384]{2,1,0:T(1,128)S(1)}, f32[18,1,384]{2,1,0:T(1,128)S(1)}, u32[]{:S(2)}, u32[]{:S(2)}) collective-permute-start(f32[18,1,384]{2,1,0:T(1,128)S(1)} %get-tuple-element.9), channel_id=1, source_target_pairs={{1,0},{2,1},{3,2},{4,3},{5,4},{6,5},{7,6},{9,8},{10,9},{11,10},{12... | collective-permute-start | bytes 82952 | tf_op jit(solution)/shard_map/ppermute | solution.py:20
  38.1 3.9 %collective-permute-start.3 = (f32[18,1,384]{2,1,0:T(1,128)S(1)}, f32[18,1,384]{2,1,0:T(1,128)S(1)}, u32[]{:S(2)}, u32[]{:S(2)}) collective-permute-start(f32[18,1,384]{2,1,0:T(1,128)S(1)} %get-tuple-element.8), channel_id=1, source_target_pairs={{0,1},{1,2},{2,3},{3,4},{4,5},{5,6},{6,7},{8,9},{9,10},{10,11},{11... | collective-permute-start | bytes 82952 | tf_op jit(solution)/shard_map/ppermute | solution.py:18
where the time goes:
time: 88.1 us; the launch traced here: 87.5 us
  blocking collectives  41.2 us (47%)
  waiting for transfers between devices  16.2 us (18%)
  starting transfers between devices  14.5 us (16%)
  other arithmetic  4.98 us (6%)
  local copies, waits for them, and re-layouts  4.87 us (6%)
  matrix products  3.05 us (3%)
  between operations  2.71 us (3%)
    psum x1, blocking collectives, shards(): total_sum = lax.psum(local_sum, ('px', 'py'))  41.2 us
    all_to_all x1, waiting for transfers between devices, shards(): lax.all_to_all(scaled, ('px', 'py'), split_axis=1, concat_axis=1, tiled=T...  10.4 us
    all_to_all x1, starting transfers between devices, shards(): lax.all_to_all(scaled, ('px', 'py'), split_axis=1, concat_axis=1, tiled=T...  7.33 us
    ppermute x2, waiting for transfers between devices, with_halo(): lax.ppermute(head, axis, [((i + 1) % count, i) for i in range(ends)])  4.95 us
    ppermute x2, starting transfers between devices, with_halo(): lax.ppermute(tail, axis, [(i, (i + 1) % count) for i in range(ends)])  4.57 us
    ppermute x2, starting transfers between devices, with_halo(): lax.ppermute(head, axis, [((i + 1) % count, i) for i in range(ends)])  2.59 us
    reshape x1, local copies, waits for them, and re-layouts, plane_table(): jnp.einsum('ux,vy->uvxy', across_x, across_y).reshape(CX * CY, CX * CY)  2.34 us
    reduce_sum x1, other arithmetic, shards(): local_sum = jnp.sum(residual * residual)  1.91 us
  transfers between devices with their start and end apart: 5, of which 3 were waited for; matrix products, arithmetic and copies ran while one was open for 4% of the time, Pallas kernels for 0%

commit v1 on v0

--- a/solution.py
+++ b/solution.py
@@ -85,7 +85,10 @@
     beside = beside + padded[1:-1, 1:-1, 2:] + padded[1:-1, 1:-1, :-2]
     residual = right_side - (6.0 * decoded - beside)
     local_sum = jnp.sum(residual * residual)
-    total_sum = lax.psum(local_sum, ("px", "py"))
+    parts = lax.all_to_all(
+        jnp.broadcast_to(local_sum, (peers,)), ("px", "py"), split_axis=0, concat_axis=0, tiled=True
+    )
+    total_sum = jnp.sum(parts)
     cell_count = decoded.shape[0] * decoded.shape[1] * decoded.shape[2] * count_x * count_y
     rms = jnp.sqrt(total_sum / cell_count + 1e-06)
     return (decoded, residual, rms)

time: 88.1 us -> 60.6 us (0.69)
  blocking collectives: 41.2 us -> 12.6 us
    psum x1 -> x0, blocking collectives: 41.2 us -> none  [shards(): total_sum = lax.psum(local_sum, ('px', 'py'))]
    all_to_all x0 -> x1, blocking collectives: none -> 12.6 us  [shards(): lax.all_to_all(jnp.broadcast_to(local_sum, (peers,)), ('px', 'py'), split...]
  transfers between devices with their start and end apart: 5 -> 5, of which waited for: 3 -> 3; matrix products, arithmetic and copies ran while one was open for 4% -> 6% of each run, Pallas kernels for 0% -> 0%
where the time goes in v1:
time: 60.6 us; the launch traced here: 60.1 us
  waiting for transfers between devices  16.2 us (27%)
  starting transfers between devices  14.5 us (24%)
  blocking collectives  12.6 us (21%)
  other arithmetic  5.61 us (9%)
  local copies, waits for them, and re-layouts  5.52 us (9%)
  matrix products  3.05 us (5%)
  between operations  2.71 us (4%)
    all_to_all x1, blocking collectives, shards(): lax.all_to_all(jnp.broadcast_to(local_sum, (peers,)), ('px', 'py'), split...  12.6 us
    all_to_all x1, waiting for transfers between devices, shards(): lax.all_to_all(scaled, ('px', 'py'), split_axis=1, concat_axis=1, tiled=T...  10.4 us
    all_to_all x1, starting transfers between devices, shards(): lax.all_to_all(scaled, ('px', 'py'), split_axis=1, concat_axis=1, tiled=T...  7.33 us
    ppermute x2, waiting for transfers between devices, with_halo(): lax.ppermute(head, axis, [((i + 1) % count, i) for i in range(ends)])  4.95 us
    ppermute x2, starting transfers between devices, with_halo(): lax.ppermute(tail, axis, [(i, (i + 1) % count) for i in range(ends)])  4.57 us
    ppermute x2, starting transfers between devices, with_halo(): lax.ppermute(head, axis, [((i + 1) % count, i) for i in range(ends)])  2.59 us
    reshape x1, local copies, waits for them, and re-layouts, plane_table(): jnp.einsum('ux,vy->uvxy', across_x, across_y).reshape(CX * CY, CX * CY)  2.34 us
    reduce_sum x1, other arithmetic, shards(): local_sum = jnp.sum(residual * residual)  1.91 us
  transfers between devices with their start and end apart: 5, of which 3 were waited for; matrix products, arithmetic and copies ran while one was open for 6% of the time, Pallas kernels for 0%

profile of v1, /device:TPU:0, one launch (start us, length us, event | category | flops | bytes accessed | tf_op | source)
XLA Modules:
  0.0 60.1 jit_solution(8100641944957439696)
XLA Ops:
  0.7 0.7 %multiply_exponential_fusion = f32[3,768]{1,0:T(4,128)S(1)} fusion(s32[3,768]{1,0:T(4,128)} %param.4), kind=kLoop, calls=%fused_computation.50 | loop fusion | flops 4608 | bytes 18432 | tf_op jit(solution)/shard_map/exp2 | solution.py:66
  1.4 0.1 reshape.522
  1.5 1.1 %reshape.527 = f32[12,12288]{1,0:T(8,128)S(1)} convert(bf16[12,12288]{1,0:T(8,128)(2,1)} %param.3) | non-fusion elementwise | flops 147456 | bytes 884736 | tf_op jit(solution)/shard_map/reshape | solution.py:71
  2.5 0.2 copy.50
  2.7 0.3 fusion.15
  3.0 0.1 fusion.1
  3.1 0.8 %copy.41 = bf16[12,32,384]{2,0,1:T(8,128)(2,1)} copy(bf16[12,32,384]{2,1,0:T(8,128)(2,1)S(1)} %fusion.1) | data formatting | bytes 589824 | tf_op jit(solution)/shard_map/convert_element_type | solution.py:71
  3.9 7.3 %all-to-all-start = ((bf16[12,32,384]{2,0,1:T(8,128)(2,1)}), bf16[12,32,384]{2,0,1:T(8,128)(2,1)S(1)}, u32[]{:S(2)}, u32[]{:S(2)}) async-start(bf16[12,32,384]{2,0,1:T(8,128)(2,1)} %copy.41), calls=%async_computation | async-start | bytes 786432 | tf_op jit(solution)/shard_map/all_to_all | solution.py:74
  11.3 0.1 multiply_select_fusion
  11.5 0.1 multiply_select_fusion.1
  11.6 0.3 multiply_bitcast_fusion
  11.9 2.3 %reshape.530 = f32[384,384,1]{1,0,2:T(8,128)} reshape(f32[16,24,16,24]{3,2,1,0:T(8,128)S(1)} %multiply_bitcast_fusion) | data formatting | bytes 1179648 | tf_op jit(solution)/shard_map/reshape | solution.py:40
  14.3 10.4 %all-to-all-done = bf16[12,32,384]{2,0,1:T(8,128)(2,1)S(1)} async-done(((bf16[12,32,384]{2,0,1:T(8,128)(2,1)}), bf16[12,32,384]{2,0,1:T(8,128)(2,1)S(1)}, u32[]{:S(2)}, u32[]{:S(2)}) %all-to-all-start) | async-done | bytes 294944 | tf_op jit(solution)/shard_map/all_to_all | solution.py:74
  24.7 1.8 %convolution_bitcast_fusion.1 = f32[32,12,384]{2,0,1:T(8,128)S(1)} fusion(f32[384,384,1]{1,0,2:T(8,128)} %reshape.530, bf16[12,32,384]{2,0,1:T(8,128)(2,1)S(1)} %all-to-all-done), kind=kOutput, calls=%fused_computation.4 | convolution fusion | flops 679477248 | bytes 1474560 | tf_op jit(solution)/shard_map/zpc,cv->zpv/dot_general | solution.py:53
  26.5 0.4 copy.43
  26.9 0.1 reshape.525
  27.0 0.9 %convolution_bitcast_fusion = f32[384,3,128]{0,2,1:T(8,128)S(1)} fusion(f32[3,128,384]{2,1,0:T(8,128)S(1)} %reshape.525, f32[128]{0:T(128)S(1)} %get-tuple-element.27, f32[128]{0:T(128)S(1)} %get-tuple-element.25, f32[128]{0:T(128)S(1)} %get-tuple-element.24, s32[128]{0:T(128)S(1)} %get-tuple-element.26), kind=kOutput, calls=%fused_computation.3 | convolution fusion | flops 226574336 | bytes 1181696 | tf_op jit(solution)/shard_map/nzq,zw->qnw/dot_general | solution.py:78
  27.9 0.1 fusion.54
  28.0 0.1 copy.46
  28.1 1.5 %collective-permute-start.1 = (f32[1,24,384]{2,1,0:T(8,128)S(1)}, f32[1,24,384]{2,1,0:T(8,128)S(1)}, u32[]{:S(2)}, u32[]{:S(2)}) collective-permute-start(f32[1,24,384]{2,1,0:T(8,128)S(1)} %copy.46), channel_id=1, source_target_pairs={{0,8},{8,16},{16,24},{1,9},{9,17},{17,25},{2,10},{10,18},{18,26},{... | collective-permute-start | bytes 110600 | tf_op jit(solution)/shard_map/ppermute | solution.py:18
  29.6 0.3 copy.44
  29.9 0.3 reshape.526
  30.3 0.0 copy-start
  30.3 0.1 copy.45
  30.4 1.3 %collective-permute-start = (f32[1,24,384]{2,1,0:T(8,128)S(1)}, f32[1,24,384]{2,1,0:T(8,128)S(1)}, u32[]{:S(2)}, u32[]{:S(2)}) collective-permute-start(f32[1,24,384]{2,1,0:T(8,128)S(1)} %copy.45), channel_id=1, source_target_pairs={{8,0},{16,8},{24,16},{9,1},{17,9},{25,17},{10,2},{18,10},{26,18},{... | collective-permute-start | bytes 110600 | tf_op jit(solution)/shard_map/ppermute | solution.py:20
  31.7 0.0 collective-permute-done.1
  31.7 0.0 copy-start.1
  31.8 4.9 %collective-permute-done = f32[1,24,384]{2,1,0:T(8,128)S(1)} collective-permute-done((f32[1,24,384]{2,1,0:T(8,128)S(1)}, f32[1,24,384]{2,1,0:T(8,128)S(1)}, u32[]{:S(2)}, u32[]{:S(2)}) %collective-permute-start) | collective-permute-done | bytes 36896 | tf_op jit(solution)/shard_map/ppermute | solution.py:20
  36.8 1.3 %collective-permute-start.2 = (f32[18,1,384]{2,1,0:T(1,128)S(1)}, f32[18,1,384]{2,1,0:T(1,128)S(1)}, u32[]{:S(2)}, u32[]{:S(2)}) collective-permute-start(f32[18,1,384]{2,1,0:T(1,128)S(1)} %get-tuple-element.9), channel_id=1, source_target_pairs={{1,0},{2,1},{3,2},{4,3},{5,4},{6,5},{7,6},{9,8},{10,9},{11,10},{12... | collective-permute-start | bytes 82952 | tf_op jit(solution)/shard_map/ppermute | solution.py:20
  38.1 3.0 %collective-permute-start.3 = (f32[18,1,384]{2,1,0:T(1,128)S(1)}, f32[18,1,384]{2,1,0:T(1,128)S(1)}, u32[]{:S(2)}, u32[]{:S(2)}) collective-permute-start(f32[18,1,384]{2,1,0:T(1,128)S(1)} %get-tuple-element.8), channel_id=1, source_target_pairs={{0,1},{1,2},{2,3},{3,4},{4,5},{5,6},{6,7},{8,9},{9,10},{10,11},{11... | collective-permute-start | bytes 82952 | tf_op jit(solution)/shard_map/ppermute | solution.py:18
  41.1 0.0 collective-permute-done.2
  41.1 0.8 %collective-permute-done.3 = f32[18,1,384]{2,1,0:T(1,128)S(1)} collective-permute-done((f32[18,1,384]{2,1,0:T(1,128)S(1)}, f32[18,1,384]{2,1,0:T(1,128)S(1)}, u32[]{:S(2)}, u32[]{:S(2)}) %collective-permute-start.3) | collective-permute-done | bytes 27680 | tf_op jit(solution)/shard_map/ppermute | solution.py:18
  41.9 0.6 select_maximum_fusion
  42.5 0.0 copy-done
  42.5 0.0 copy-done.1
  42.5 1.9 %multiply_reduce_fusion = (f32[]{:T(128)}, f32[16,24,384]{2,1,0:T(8,128)}) fusion(f32[16,24,384]{2,1,0:T(8,128)S(1)} %copy-done.1, f32[18,26,386]{2,1,0:T(8,128)S(1)} %select_maximum_fusion, f32[18,24,384]{2,1,0:T(8,128)S(1)} %constant_dynamic-update-slice_fusion, f32[18,1,384]{2,1,0:T(1,128)S(1)} %collective-permute-done.3, ...), kind=kLoop, calls=%fused_computation.21 | loop fusion | flops 2064383 | bytes 3741700 | tf_op jit(solution)/shard_map/reduce_sum | solution.py:87
  44.4 0.7 %broadcast_in_dim.73 = f32[32,1,1]{2,1,0:T(1,128)S(1)} broadcast(f32[]{:T(128)} %get-tuple-element.6), dimensions={} | broadcast | bytes 132 | tf_op jit(solution)/shard_map/broadcast_in_dim | solution.py:89
  45.1 12.6 %all_to_all.11 = f32[32,1,1]{2,1,0:T(1,128)S(1)} all-to-all(f32[32,1,1]{2,1,0:T(1,128)S(1)} %broadcast_in_dim.73), channel_id=1, replica_groups=mesh['px'=4,'py'=8] {'px','py'}, dimensions={0} | all-to-all | bytes 256 | tf_op jit(solution)/shard_map/all_to_all | solution.py:88
  57.7 0.6 %reduce_sum.19 = f32[]{:T(128)} reduce(f32[32,1,1]{2,1,0:T(1,128)S(1)} %all_to_all.11, f32[]{:T(128)} %constant.201.clone.1), dimensions={0,1,2}, to_apply=%region_1.2 | reduce | flops 31 | bytes 136 | tf_op jit(solution)/shard_map/reduce_sum | solution.py:91
  (12 shorter events, 0.2 us)
Async XLA Ops:
  3.9 20.8 %all-to-all-start = ((bf16[12,32,384]{2,0,1:T(8,128)(2,1)}), bf16[12,32,384]{2,0,1:T(8,128)(2,1)S(1)}, u32[]{:S(2)}, u32[]{:S(2)}) async-start(bf16[12,32,384]{2,0,1:T(8,128)(2,1)} %copy.41), calls=%async_computation | async-start | bytes 786432 | tf_op jit(solution)/shard_map/all_to_all | solution.py:74
  28.1 3.6 %collective-permute-start.1 = (f32[1,24,384]{2,1,0:T(8,128)S(1)}, f32[1,24,384]{2,1,0:T(8,128)S(1)}, u32[]{:S(2)}, u32[]{:S(2)}) collective-permute-start(f32[1,24,384]{2,1,0:T(8,128)S(1)} %copy.46), channel_id=1, source_target_pairs={{0,8},{8,16},{16,24},{1,9},{9,17},{17,25},{2,10},{10,18},{18,26},{... | collective-permute-start | bytes 110600 | tf_op jit(solution)/shard_map/ppermute | solution.py:18
  30.3 12.3 %copy-start = (f32[16,24,384]{2,1,0:T(8,128)}, f32[16,24,384]{2,1,0:T(8,128)S(1)}, u32[]{:S(2)}) copy-start(f32[16,24,384]{2,1,0:T(8,128)S(1)} %reshape.526) | copy-start | bytes 1769476
  30.4 6.3 %collective-permute-start = (f32[1,24,384]{2,1,0:T(8,128)S(1)}, f32[1,24,384]{2,1,0:T(8,128)S(1)}, u32[]{:S(2)}, u32[]{:S(2)}) collective-permute-start(f32[1,24,384]{2,1,0:T(8,128)S(1)} %copy.45), channel_id=1, source_target_pairs={{8,0},{16,8},{24,16},{9,1},{17,9},{25,17},{10,2},{18,10},{26,18},{... | collective-permute-start | bytes 110600 | tf_op jit(solution)/shard_map/ppermute | solution.py:20
  31.7 10.8 %copy-start.1 = (f32[16,24,384]{2,1,0:T(8,128)S(1)}, f32[16,24,384]{2,1,0:T(8,128)}, u32[]{:S(2)}) copy-start(f32[16,24,384]{2,1,0:T(8,128)} %param.5) | copy-start | bytes 1769476
  36.8 4.3 %collective-permute-start.2 = (f32[18,1,384]{2,1,0:T(1,128)S(1)}, f32[18,1,384]{2,1,0:T(1,128)S(1)}, u32[]{:S(2)}, u32[]{:S(2)}) collective-permute-start(f32[18,1,384]{2,1,0:T(1,128)S(1)} %get-tuple-element.9), channel_id=1, source_target_pairs={{1,0},{2,1},{3,2},{4,3},{5,4},{6,5},{7,6},{9,8},{10,9},{11,10},{12... | collective-permute-start | bytes 82952 | tf_op jit(solution)/shard_map/ppermute | solution.py:20
  38.1 3.9 %collective-permute-start.3 = (f32[18,1,384]{2,1,0:T(1,128)S(1)}, f32[18,1,384]{2,1,0:T(1,128)S(1)}, u32[]{:S(2)}, u32[]{:S(2)}) collective-permute-start(f32[18,1,384]{2,1,0:T(1,128)S(1)} %get-tuple-element.8), channel_id=1, source_target_pairs={{0,1},{1,2},{2,3},{3,4},{4,5},{5,6},{6,7},{8,9},{9,10},{10,11},{11... | collective-permute-start | bytes 82952 | tf_op jit(solution)/shard_map/ppermute | solution.py:18

commit v2 on v0

v2 whole, which is shorter than its diff:
```python
import functools

import jax
import jax.numpy as jnp
import numpy as np
from jax import lax
from jax.experimental import pallas as pl
from jax.experimental.pallas import tpu as pltpu
from jax.sharding import PartitionSpec as P

AXES = ("px", "py")
LANES = 128
ROWS = 56
TAIL = 48
LAYERS = 12
GROUP = 4


def basis4():
    a = np.arange(4)[:, None]
    i = np.arange(4)[None, :]
    weight = np.where(a == 0, np.sqrt(0.25), np.sqrt(0.5))
    return weight * np.cos(np.pi * (2 * i + 1) * a / 8)


def halves(table):
    table = table.astype(np.float32)
    high = table.astype(jnp.bfloat16)
    low = (table - high.astype(np.float32)).astype(jnp.bfloat16)
    return high, low


def plane(cx, cy):
    across_x = np.kron(np.eye(cx // 4), basis4())
    across_y = np.kron(np.eye(cy // 4), basis4())
    return np.kron(across_x, across_y)


def edge_table(cx, cy):
    full = plane(cx, cy).reshape(cx * cy, cx, cy)
    x_high, x_low = full[:, cx - 1, :], full[:, 0, :]
    y_high, y_low = full[:, :, cy - 1], full[:, :, 0]
    table = np.concatenate([x_high, x_low, y_high, y_low, x_high, x_low], axis=1)
    return np.concatenate(halves(table), axis=1)


def spread_table(cx, cy, per):
    quarter = cy // 4
    blocks = cx // 4 * quarter
    cell = np.arange(cx * cy)
    block = cell // cy // 4 * quarter + cell % cy // 4
    same = (np.arange(per * blocks) % blocks)[:, None] == block[None, :]
    return same.astype(jnp.bfloat16)


def depth_table():
    basis = basis4()
    table = np.zeros((5, GROUP, LAYERS, GROUP, ROWS))
    for s in range(GROUP):
        for point in range(LAYERS):
            block, k = divmod(point, 4)
            for a in range(4):
                layer = 4 * block + a
                for t in range(3):
                    table[t, s, point, s, 16 * t + layer] = basis[a, k]
                table[3, s, point, s, 16 * block + 12 + a] = basis[a, k]
                table[4, s, point, s, TAIL + a] = basis[a, k]
    return np.concatenate(halves(table.reshape(5 * GROUP * LAYERS, GROUP * ROWS)), axis=0)


def plane_windows(cx, cy):
    flipped = plane(cx, cy).T
    half = cx * cy // 2
    width = 2 * LANES
    first = flipped[:half, :width]
    second = flipped[half:, cx * cy - width :]
    return np.stack(halves(np.stack([first, second])))


def pick_table(cx, cy):
    edges = 2 * cy + 2 * cx
    table = np.zeros((edges, 2 * LANES), np.float32)
    for k in range(2 * cy):
        table[k, k] = 1
        table[k, edges + k] = 1
    for k in range(2 * cx):
        table[2 * cy + k, 2 * cy + k] = 1
        for block in range(3):
            table[2 * cy + k, LANES + 2 * cx * block + k] = 1
    return table.astype(jnp.bfloat16)


def send_kernel(
    count_x, count_y, cx, cy, coef_ref, exp_ref, spread_ref, edge_ref, out_ref, factor, scaled, edge
):
    peers = count_x * count_y
    patch = cx * cy
    blocks = patch // 16
    per = patch // blocks
    edges = 2 * cy + 2 * cx
    power = lax.shift_left(jnp.int32(1), exp_ref[...] + 15).astype(jnp.float32) * (2.0**-15)
    lane = lax.broadcasted_iota(jnp.int32, (per, patch), 1)
    row = lax.broadcasted_iota(jnp.int32, (per, patch), 0)
    own = (lane >= row * blocks) & (lane < (row + 1) * blocks)
    for h in range(peers // per):
        part = power[:, h * patch : (h + 1) * patch]
        stacked = [
            jnp.where(own, jnp.broadcast_to(part[b : b + 1], (per, patch)), 0.0) for b in range(3)
        ]
        left = jnp.concatenate(stacked, axis=0).astype(jnp.bfloat16)
        factor[h * 3 * per : (h + 1) * 3 * per, :] = jnp.dot(
            left, spread_ref[...], preferred_element_type=jnp.float32
        )
    layer = lax.broadcasted_iota(jnp.int32, (LAYERS, patch), 0)
    for p in range(peers):
        base = p // per * 3 * per + p % per
        rows = [
            jnp.broadcast_to(factor[base + b * per : base + b * per + 1, :], (LAYERS, patch))
            for b in range(3)
        ]
        spread = jnp.where(layer < 4, rows[0], jnp.where(layer < 8, rows[1], rows[2]))
        part = coef_ref[:, p * patch : (p + 1) * patch].astype(jnp.float32) * spread
        part = part.astype(jnp.bfloat16)
        scaled[p, 0:LAYERS, :] = part
        for t in range(3):
            out_ref[p, 16 * t : 16 * t + LAYERS, :] = part[:, t * LANES : (t + 1) * LANES]
    found = jnp.dot(
        scaled[...].reshape(peers * 16, patch), edge_ref[...], preferred_element_type=jnp.float32
    )
    edge[...] = (found[:, :LANES] + found[:, LANES:]).reshape(peers, 16, LANES)
    lane = lax.broadcasted_iota(jnp.int32, (16, LANES), 1)
    from_left = (lane < cy) | ((lane >= edges) & (lane < edges + cy))
    from_right = ((lane >= cy) & (lane < 2 * cy)) | (lane >= edges + cy)
    from_below = (lane >= 2 * cy) & (lane < 2 * cy + cx)
    nothing = jnp.zeros((16, LANES), jnp.float32)
    for p in range(peers):
        i, j = divmod(p, count_y)
        left = edge[p - count_y] if i > 0 else nothing
        right = edge[p + count_y] if i < count_x - 1 else nothing
        below = edge[p - 1] if j > 0 else nothing
        above = edge[p + 1] if j < count_y - 1 else nothing
        value = jnp.where(
            from_left, left, jnp.where(from_right, right, jnp.where(from_below, below, above))
        )
        high = value.astype(jnp.bfloat16).astype(jnp.float32)
        low = value - high
        tile = jnp.where(lane < edges, high, low)
        for t in range(3):
            out_ref[p, 16 * t + LAYERS : 16 * t + 16, :] = tile[4 * t : 4 * t + 4].astype(
                jnp.bfloat16
            )
        wide = lane[:4]
        first = pltpu.roll(low[0:8], LANES - 2 * cy, 1)[0:4]
        second = pltpu.roll(low[0:8], LANES - 2 * cy + 2 * cx, 1)[4:8]
        third = pltpu.roll(low[8:16], (4 * cx - 2 * cy) % LANES, 1)[0:4]
        tail = jnp.where(wide < 2 * cx, first, jnp.where(wide < 4 * cx, second, third))
        tail = jnp.where(wide < 6 * cx, tail, 0.0)
        tail = jnp.concatenate([tail, jnp.zeros((4, LANES), jnp.float32)], axis=0)
        out_ref[p, TAIL:ROWS, :] = tail.astype(jnp.bfloat16)


def split(value):
    high = value.astype(jnp.bfloat16)
    return high, (value - high.astype(jnp.float32)).astype(jnp.bfloat16)


def receive_kernel(
    cx, cy, got_ref, right_ref, depth_ref, plane_ref, pick_ref, dec_ref, res_ref, sum_ref,
    high_ref, low_ref, edge_ref,
):
    peers = got_ref.shape[0]
    depth = peers * LAYERS
    patch = cx * cy
    count = GROUP * LAYERS
    contract = (((1,), (1,)), ((), ()))
    row = lax.broadcasted_iota(jnp.int32, (count, LANES), 0)
    lane = lax.broadcasted_iota(jnp.int32, (count, LANES), 1)
    third = 2 * cx
    block = row // 4 % 3
    in_block = (lane >= block * third) & (lane < (block + 1) * third)
    for g in range(0, peers // GROUP, 2):
        messages = [
            got_ref[GROUP * h : GROUP * (h + 1)].reshape(GROUP * ROWS, LANES) for h in (g, g + 1)
        ]
        both = jnp.dot(
            depth_ref[...], jnp.concatenate(messages, axis=1), preferred_element_type=jnp.float32
        )
        both = both[: 5 * count] + both[5 * count :]
        for h in range(2):
            at = (g + h) * count
            for t in range(5):
                value = both[t * count : (t + 1) * count, h * LANES : (h + 1) * LANES]
                if t == 4:
                    value = jnp.where(in_block, value, 0.0)
                high, low = split(value)
                high_ref[at : at + count, t * LANES : (t + 1) * LANES] = high
                low_ref[at : at + count, t * LANES : (t + 1) * LANES] = low

    def across(table, ref, start):
        return lax.dot_general(
            table, ref[:, start : start + 2 * LANES], contract, preferred_element_type=jnp.float32
        )

    for w, start in enumerate((0, patch - 2 * LANES)):
        found = across(plane_ref[0, w], high_ref, start) + across(plane_ref[0, w], low_ref, start)
        found = found + across(plane_ref[1, w], high_ref, start)
        dec_ref[w * cx // 2 : (w + 1) * cx // 2] = found.reshape(cx // 2, cy, depth)
    edge_ref[...] = across(pick_ref[...], high_ref, patch) + across(pick_ref[...], low_ref, patch)

    row = lax.broadcasted_iota(jnp.int32, (cy, depth), 0)
    lane = lax.broadcasted_iota(jnp.int32, (cy, depth), 1)
    total = jnp.zeros((8, LANES), jnp.float32)
    for x in range(cx):
        here = dec_ref[x]
        beside = dec_ref[x - 1] if x > 0 else edge_ref[0:cy]
        beside = beside + (dec_ref[x + 1] if x < cx - 1 else edge_ref[cy : 2 * cy])
        low = edge_ref[2 * cy + x : 2 * cy + x + 1]
        high = edge_ref[2 * cy + cx + x : 2 * cy + cx + x + 1]
        beside = beside + jnp.where(row == 0, low, pltpu.roll(here, 1, 0))
        beside = beside + jnp.where(row == cy - 1, high, pltpu.roll(here, cy - 1, 0))
        beside = beside + jnp.where(lane == 0, 0.0, pltpu.roll(here, 1, 1))
        beside = beside + jnp.where(lane == depth - 1, 0.0, pltpu.roll(here, depth - 1, 1))
        left = right_ref[x] - (6.0 * here - beside)
        res_ref[x] = left
        square = left * left
        for r in range(0, cy, 8):
            for c in range(0, depth, LANES):
                total = total + square[r : r + 8, c : c + LANES]
    total = jnp.sum(total, axis=0, keepdims=True)
    sum_ref[...] = jnp.broadcast_to(total[None], sum_ref.shape)


def shards(count_x, count_y, coefficients, exponents, right_side):
    peers = count_x * count_y
    cx, cy, depth = right_side.shape
    patch = cx * cy
    per = 16
    vmem = pl.BlockSpec(memory_space=pltpu.VMEM)
    messages = pl.pallas_call(
        functools.partial(send_kernel, count_x, count_y, cx, cy),
        out_shape=jax.ShapeDtypeStruct((peers, ROWS, LANES), jnp.bfloat16),
        in_specs=[vmem] * 4,
        out_specs=vmem,
        scratch_shapes=[
            pltpu.VMEM((peers * 3, patch), jnp.float32),
            pltpu.VMEM((peers, 16, patch), jnp.bfloat16),
            pltpu.VMEM((peers, 16, LANES), jnp.float32),
        ],
        name="send",
    )(
        coefficients,
        exponents,
        jnp.asarray(spread_table(cx, cy, per)),
        jnp.asarray(edge_table(cx, cy)),
    )
    got = lax.all_to_all(messages, AXES, split_axis=0, concat_axis=0, tiled=True)
    decoded, residual, parts = pl.pallas_call(
        functools.partial(receive_kernel, cx, cy),
        out_shape=(
            jax.ShapeDtypeStruct((cx, cy, depth), jnp.float32),
            jax.ShapeDtypeStruct((cx, cy, depth), jnp.float32),
            jax.ShapeDtypeStruct((peers, 1, LANES), jnp.float32),
        ),
        in_specs=[vmem] * 5,
        out_specs=(vmem, vmem, vmem),
        scratch_shapes=[
            pltpu.VMEM((depth, 5 * LANES), jnp.bfloat16),
            pltpu.VMEM((depth, 5 * LANES), jnp.bfloat16),
            pltpu.VMEM((2 * cx + 2 * cy, depth), jnp.float32),
        ],
        name="receive",
    )(
        got,
        right_side,
        jnp.asarray(depth_table()),
        jnp.asarray(plane_windows(cx, cy)),
        jnp.asarray(pick_table(cx, cy)),
    )
    parts = lax.all_to_all(parts, AXES, split_axis=0, concat_axis=0, tiled=True)
    rms = jnp.sqrt(jnp.sum(parts) / (patch * depth * peers) + 1e-6)
    return (decoded, residual, rms)


def solution(mesh):
    return jax.shard_map(
        functools.partial(shards, mesh.shape["px"], mesh.shape["py"]),
        mesh=mesh,
        in_specs=(P(AXES, None), P(AXES, None), P("px", "py", None)),
        out_specs=(P("px", "py", None), P("px", "py", None), P()),
        check_vma=False,
    )
```

time: 88.1 us -> 41.4 us (0.47)
  waiting for transfers between devices: 16.2 us -> 0 us
  starting transfers between devices: 14.5 us -> 0 us
  blocking collectives: 41.2 us -> 32 us
  Pallas kernels: 0 us -> 6 us
  local copies, waits for them, and re-layouts: 4.87 us -> 0 us
  other arithmetic: 4.98 us -> 0.63 us
  matrix products: 3.05 us -> 0 us
    psum x1 -> x0, blocking collectives: 41.2 us -> none  [shards(): total_sum = lax.psum(local_sum, ('px', 'py'))]
    all_to_all x0 -> x2, blocking collectives: none -> 32 us  [the longest x1 22.3 us: shards(): lax.all_to_all(messages, AXES, split_axis=0, concat_axis=0, tiled=True)]
    all_to_all x1 -> x0, waiting for transfers between devices: 10.4 us -> none  [shards(): lax.all_to_all(scaled, ('px', 'py'), split_axis=1, concat_axis=1, tiled=T...]
    all_to_all x1 -> x0, starting transfers between devices: 7.33 us -> none  [shards(): lax.all_to_all(scaled, ('px', 'py'), split_axis=1, concat_axis=1, tiled=T...]
    ppermute x4 -> x0, starting transfers between devices: 7.16 us -> none  [the longest x2 4.57 us: with_halo(): lax.ppermute(tail, axis, [(i, (i + 1) % count) for i in range(ends)])]
    pallas_call x0 -> x2, Pallas kernels: none -> 6 us  [the longest x1 3.45 us: shards(): pl.pallas_call(functools.partial(receive_kernel, cx, cy), out_shape=(jax....]
    ppermute x4 -> x0, waiting for transfers between devices: 5.78 us -> none  [the longest x2 4.95 us: with_halo(): lax.ppermute(head, axis, [((i + 1) % count, i) for i in range(ends)])]
    dot_general x3 -> x0, matrix products: 3.05 us -> none  [the longest x1 1.82 us: apply_plane(): jnp.einsum('zpc,cv->zpv', layers.astype(jnp.float32), table, precision=la...]
  transfers between devices with their start and end apart: 5 -> 0, of which waited for: 3 -> 0; matrix products, arithmetic and copies ran while one was open for 4% -> 0% of each run, Pallas kernels for 0% -> 0%
where the time goes in v2:
time: 41.4 us; the launch traced here: 41.1 us
  blocking collectives  32 us (77%)
  Pallas kernels  6 us (14%)
  between operations  2.45 us (6%)
  other arithmetic  0.63 us (2%)
    all_to_all x1, blocking collectives, shards(): lax.all_to_all(messages, AXES, split_axis=0, concat_axis=0, tiled=True)  22.3 us
    all_to_all x1, blocking collectives, shards(): parts = lax.all_to_all(parts, AXES, split_axis=0, concat_axis=0, tiled=True)  9.72 us
    pallas_call x1, Pallas kernels, shards(): pl.pallas_call(functools.partial(receive_kernel, cx, cy), out_shape=(jax....  3.45 us
    pallas_call x1, Pallas kernels, shards(): pl.pallas_call(functools.partial(send_kernel, count_x, count_y, cx, cy),...  2.56 us

profile of v2, /device:TPU:0, one launch (start us, length us, event | category | flops | bytes accessed | tf_op | source)
XLA Modules:
  0.0 41.1 jit_solution(8129005244008645511)
XLA Ops:
  0.6 2.6 %send.1 = bf16[32,56,128]{2,1,0:T(8,128)(2,1)} custom-call(bf16[12,12288]{1,0:T(8,128)(2,1)} %coef_ref.1, s32[3,768]{1,0:T(4,128)} %exp_ref.1, bf16[384,384]{1,0:T(8,128)(2,1)} %constant.17.clone.spread_ref, bf16[384,256]{1,0:T(8,128)(2,1)} %constant.18.clone.edge_ref), custom_call_target="tpu_custom_call" | custom-call | tf_op jit(solution)/shard_map/send/pallas_call | solution.py:239
  3.2 22.3 %all_to_all.10.got_ref = bf16[32,56,128]{2,1,0:T(8,128)(2,1)} all-to-all(bf16[32,56,128]{2,1,0:T(8,128)(2,1)} %send.1), channel_id=1, replica_groups=mesh['px'=4,'py'=8] {'px','py'}, dimensions={0} | all-to-all | bytes 917504 | tf_op jit(solution)/shard_map/all_to_all | solution.py:256
  25.5 3.4 %receive.1 = (f32[16,24,384]{2,1,0:T(8,128)}, f32[16,24,384]{2,1,0:T(8,128)}, f32[32,1,128]{2,1,0:T(1,128)}) custom-call(bf16[32,56,128]{2,1,0:T(8,128)(2,1)} %all_to_all.10.got_ref, f32[16,24,384]{2,1,0:T(8,128)} %right_ref.1, bf16[480,224]{1,0:T(8,128)(2,1)} %constant.19.clone.depth_ref, bf16[2,2,192,256]{3,2,1,0:T(8,128)(2,1)} %constant.20.clone.plane_ref, ...), custom_call_target="tpu_custom_call" | custom-call | tf_op jit(solution)/shard_map/receive/pallas_call | solution.py:257
  28.9 9.7 %all_to_all.11 = f32[32,1,128]{2,1,0:T(1,128)S(1)} all-to-all(f32[32,1,128]{2,1,0:T(1,128)} %get-tuple-element.8), channel_id=1, replica_groups=mesh['px'=4,'py'=8] {'px','py'}, dimensions={0} | all-to-all | bytes 32768 | tf_op jit(solution)/shard_map/all_to_all | solution.py:279
  38.6 0.6 %reduce_sum.9 = f32[]{:T(128)} reduce(f32[32,1,128]{2,1,0:T(1,128)S(1)} %all_to_all.11, f32[]{:T(128)} %constant.6.clone.1), dimensions={0,1,2}, to_apply=%region_0.0 | reduce | flops 4095 | bytes 16392 | tf_op jit(solution)/shard_map/reduce_sum | solution.py:280

commit v3 on v2

--- a/solution.py
+++ b/solution.py
@@ -14,6 +14,10 @@
 TAIL = 48
 LAYERS = 12
 GROUP = 4
+
+
+def exchange(array):
+    return lax.all_to_all(array, AXES, split_axis=0, concat_axis=0, tiled=True)
 
 
 def basis4():
@@ -91,8 +95,18 @@
 
 
 def send_kernel(
-    count_x, count_y, cx, cy, coef_ref, exp_ref, spread_ref, edge_ref, out_ref, factor, scaled, edge
+    count_x, count_y, cx, cy, coef_hbm, exp_hbm, spread_hbm, edge_hbm, right_hbm, table_hbm,
+    out_ref, right_ref, table_ref, coef_ref, exp_ref, spread_ref, edge_ref, factor, scaled, edge, sems,
 ):
+    pairs = [
+        (exp_hbm, exp_ref), (spread_hbm, spread_ref), (coef_hbm, coef_ref), (edge_hbm, edge_ref),
+        (right_hbm, right_ref), (table_hbm, table_ref),
+    ]
+    loads = [pltpu.make_async_copy(a, b, sems.at[n]) for n, (a, b) in enumerate(pairs)]
+    for load in loads:
+        load.start()
+    loads[0].wait()
+    loads[1].wait()
     peers = count_x * count_y
     patch = cx * cy
     blocks = patch // 16
@@ -112,6 +126,7 @@
             left, spread_ref[...], preferred_element_type=jnp.float32
         )
     layer = lax.broadcasted_iota(jnp.int32, (LAYERS, patch), 0)
+    loads[2].wait()
     for p in range(peers):
         base = p // per * 3 * per + p % per
         rows = [
@@ -124,6 +139,7 @@
         scaled[p, 0:LAYERS, :] = part
         for t in range(3):
             out_ref[p, 16 * t : 16 * t + LAYERS, :] = part[:, t * LANES : (t + 1) * LANES]
+    loads[3].wait()
     found = jnp.dot(
         scaled[...].reshape(peers * 16, patch), edge_ref[...], preferred_element_type=jnp.float32
     )
@@ -157,6 +173,15 @@
         tail = jnp.where(wide < 6 * cx, tail, 0.0)
         tail = jnp.concatenate([tail, jnp.zeros((4, LANES), jnp.float32)], axis=0)
         out_ref[p, TAIL:ROWS, :] = tail.astype(jnp.bfloat16)
+    loads[4].wait()
+    loads[5].wait()
+
+
+def receive_table(cx, cy):
+    depth = depth_table()
+    depth = np.pad(depth, ((0, 0), (0, 2 * LANES - depth.shape[1])))
+    planes = plane_windows(cx, cy).reshape(-1, 2 * LANES)
+    return np.concatenate([depth, planes, pick_table(cx, cy)], axis=0)
 
 
 def split(value):
@@ -165,8 +190,8 @@
 
 
 def receive_kernel(
-    cx, cy, got_ref, right_ref, depth_ref, plane_ref, pick_ref, dec_ref, res_ref, sum_ref,
-    high_ref, low_ref, edge_ref,
+    cx, cy, got_ref, right_ref, table_ref, dec_hbm, res_hbm, sum_ref,
+    high_ref, low_ref, edge_ref, dec_ref, res_ref, sems,
 ):
     peers = got_ref.shape[0]
     depth = peers * LAYERS
@@ -176,6 +201,10 @@
     row = lax.broadcasted_iota(jnp.int32, (count, LANES), 0)
     lane = lax.broadcasted_iota(jnp.int32, (count, LANES), 1)
     third = 2 * cx
+    half = patch // 2
+    tables = 10 * count
+    flat = [table_ref[tables + half * n : tables + half * (n + 1)] for n in range(4)]
+    pick = table_ref[tables + 4 * half :]
     block = row // 4 % 3
     in_block = (lane >= block * third) & (lane < (block + 1) * third)
     for g in range(0, peers // GROUP, 2):
@@ -183,7 +212,7 @@
             got_ref[GROUP * h : GROUP * (h + 1)].reshape(GROUP * ROWS, LANES) for h in (g, g + 1)
         ]
         both = jnp.dot(
-            depth_ref[...], jnp.concatenate(messages, axis=1), preferred_element_type=jnp.float32
+            table_ref[:tables, : GROUP * ROWS], jnp.concatenate(messages, axis=1), preferred_element_type=jnp.float32
         )
         both = both[: 5 * count] + both[5 * count :]
         for h in range(2):
@@ -201,11 +230,15 @@
             table, ref[:, start : start + 2 * LANES], contract, preferred_element_type=jnp.float32
         )
 
+    stores = []
     for w, start in enumerate((0, patch - 2 * LANES)):
-        found = across(plane_ref[0, w], high_ref, start) + across(plane_ref[0, w], low_ref, start)
-        found = found + across(plane_ref[1, w], high_ref, start)
-        dec_ref[w * cx // 2 : (w + 1) * cx // 2] = found.reshape(cx // 2, cy, depth)
-    edge_ref[...] = across(pick_ref[...], high_ref, patch) + across(pick_ref[...], low_ref, patch)
+        found = across(flat[w], high_ref, start) + across(flat[w], low_ref, start)
+        found = found + across(flat[2 + w], high_ref, start)
+        part = pl.ds(w * cx // 2, cx // 2)
+        dec_ref[part] = found.reshape(cx // 2, cy, depth)
+        stores.append(pltpu.make_async_copy(dec_ref.at[part], dec_hbm.at[part], sems.at[w]))
+        stores[-1].start()
+    edge_ref[...] = across(pick, high_ref, patch) + across(pick, low_ref, patch)
 
     row = lax.broadcasted_iota(jnp.int32, (cy, depth), 0)
     lane = lax.broadcasted_iota(jnp.int32, (cy, depth), 1)
@@ -226,8 +259,22 @@
         for r in range(0, cy, 8):
             for c in range(0, depth, LANES):
                 total = total + square[r : r + 8, c : c + LANES]
+        if x % 4 == 3:
+            part = pl.ds(x - 3, 4)
+            stores.append(
+                pltpu.make_async_copy(res_ref.at[part], res_hbm.at[part], sems.at[2 + x // 4])
+            )
+            stores[-1].start()
     total = jnp.sum(total, axis=0, keepdims=True)
     sum_ref[...] = jnp.broadcast_to(total[None], sum_ref.shape)
+    for store in stores:
+        store.wait()
+
+
+def finish_kernel(cells, parts_ref, rms_ref):
+    total = jnp.sum(parts_ref[...].reshape(-1, LANES), axis=0, keepdims=True)
+    total = jnp.sum(total, axis=1, keepdims=True)
+    rms_ref[...] = jnp.sqrt(total / cells + 1e-6)
 
 
 def shards(count_x, count_y, coefficients, exponents, right_side):
@@ -236,49 +283,71 @@
     patch = cx * cy
     per = 16
     vmem = pl.BlockSpec(memory_space=pltpu.VMEM)
-    messages = pl.pallas_call(
+    hbm = pl.BlockSpec(memory_space=pltpu.HBM)
+    tables = jnp.asarray(receive_table(cx, cy))
+    kept = [(right_side.shape, right_side.dtype), (tables.shape, tables.dtype)]
+    kept = [((peers, ROWS, LANES), jnp.bfloat16)] + kept
+    held = sum(int(np.prod(shape)) * jnp.dtype(dtype).itemsize for shape, dtype in kept)
+    near = held <= 2 << 20
+    place = pltpu.VMEM if near else jax.ShapeDtypeStruct
+    messages, right_side, tables = pl.pallas_call(
         functools.partial(send_kernel, count_x, count_y, cx, cy),
-        out_shape=jax.ShapeDtypeStruct((peers, ROWS, LANES), jnp.bfloat16),
-        in_specs=[vmem] * 4,
-        out_specs=vmem,
+        out_shape=[place(*k) for k in kept],
+        in_specs=[hbm] * 6,
+        out_specs=[vmem] * 3,
         scratch_shapes=[
+            pltpu.VMEM(coefficients.shape, coefficients.dtype),
+            pltpu.VMEM(exponents.shape, exponents.dtype),
+            pltpu.VMEM((patch, patch), jnp.bfloat16),
+            pltpu.VMEM((patch, 2 * LANES), jnp.bfloat16),
             pltpu.VMEM((peers * 3, patch), jnp.float32),
             pltpu.VMEM((peers, 16, patch), jnp.bfloat16),
             pltpu.VMEM((peers, 16, LANES), jnp.float32),
+            pltpu.SemaphoreType.DMA((6,)),
         ],
+        compiler_params=pltpu.CompilerParams(
+            vmem_limit_bytes=(64 << 20) - held - (256 << 10) if near else 48 << 20
+        ),
         name="send",
     )(
         coefficients,
         exponents,
         jnp.asarray(spread_table(cx, cy, per)),
         jnp.asarray(edge_table(cx, cy)),
+        right_side,
+        tables,
     )
-    got = lax.all_to_all(messages, AXES, split_axis=0, concat_axis=0, tiled=True)
+    got = exchange(messages)
     decoded, residual, parts = pl.pallas_call(
         functools.partial(receive_kernel, cx, cy),
         out_shape=(
             jax.ShapeDtypeStruct((cx, cy, depth), jnp.float32),
             jax.ShapeDtypeStruct((cx, cy, depth), jnp.float32),
-            jax.ShapeDtypeStruct((peers, 1, LANES), jnp.float32),
+            pltpu.VMEM((peers, 1, LANES), jnp.float32),
         ),
-        in_specs=[vmem] * 5,
-        out_specs=(vmem, vmem, vmem),
+        in_specs=[vmem] * 3,
+        out_specs=(hbm, hbm, vmem),
         scratch_shapes=[
             pltpu.VMEM((depth, 5 * LANES), jnp.bfloat16),
             pltpu.VMEM((depth, 5 * LANES), jnp.bfloat16),
             pltpu.VMEM((2 * cx + 2 * cy, depth), jnp.float32),
+            pltpu.VMEM((cx, cy, depth), jnp.float32),
+            pltpu.VMEM((cx, cy, depth), jnp.float32),
+            pltpu.SemaphoreType.DMA((2 + cx // 4,)),
         ],
+        compiler_params=pltpu.CompilerParams(vmem_limit_bytes=(12 << 20) * peers // 32),
         name="receive",
-    )(
-        got,
-        right_side,
-        jnp.asarray(depth_table()),
-        jnp.asarray(plane_windows(cx, cy)),
-        jnp.asarray(pick_table(cx, cy)),
-    )
-    parts = lax.all_to_all(parts, AXES, split_axis=0, concat_axis=0, tiled=True)
-    rms = jnp.sqrt(jnp.sum(parts) / (patch * depth * peers) + 1e-6)
-    return (decoded, residual, rms)
+    )(got, right_side, tables)
+    parts = exchange(parts)
+    rms = pl.pallas_call(
+        functools.partial(finish_kernel, patch * depth * peers),
+        out_shape=jax.ShapeDtypeStruct((1, 1), jnp.float32),
+        in_specs=[vmem],
+        out_specs=vmem,
+        compiler_params=pltpu.CompilerParams(vmem_limit_bytes=1 << 20),
+        name="finish",
+    )(parts)
+    return (decoded, residual, rms.reshape(()))
 
 
 def solution(mesh):

time: 41.4 us -> 36.6 us (0.88)
  between operations: 2.45 us -> 0.65 us
  Pallas kernels: 6 us -> 4.46 us
  blocking collectives: 32 us -> 31.2 us
  other arithmetic: 0.63 us -> 0 us
    pallas_call x1, Pallas kernels: 3.45 us -> 2.07 us  [shards(): pl.pallas_call(functools.partial(receive_kernel, cx, cy), out_shape=(jax....]
    pallas_call x1, Pallas kernels: 2.56 us -> 1.77 us  [shards(): pl.pallas_call(functools.partial(send_kernel, count_x, count_y, cx, cy),...]
    all_to_all x2, blocking collectives: 32 us -> 31.2 us  [exchange(): return lax.all_to_all(array, AXES, split_axis=0, concat_axis=0, tiled=True)]
    reduce_sum x1 -> x0, other arithmetic: 0.63 us -> none  [shards(): rms = jnp.sqrt(jnp.sum(parts) / (patch * depth * peers) + 1e-06)]
    pallas_call x0 -> x1, Pallas kernels: none -> 0.62 us  [shards(): pl.pallas_call(functools.partial(finish_kernel, patch * depth * peers), o...]
where the time goes in v3:
time: 36.6 us; the launch traced here: 36.3 us
  blocking collectives  31.2 us (85%)
  Pallas kernels  4.46 us (12%)
  between operations  0.65 us (2%)
    all_to_all x2, blocking collectives, exchange(): return lax.all_to_all(array, AXES, split_axis=0, concat_axis=0, tiled=True)  31.2 us
    pallas_call x1, Pallas kernels, shards(): pl.pallas_call(functools.partial(receive_kernel, cx, cy), out_shape=(jax....  2.07 us
    pallas_call x1, Pallas kernels, shards(): pl.pallas_call(functools.partial(send_kernel, count_x, count_y, cx, cy),...  1.77 us

profile of v3, /device:TPU:0, one launch (start us, length us, event | category | flops | bytes accessed | tf_op | source)
XLA Modules:
  0.0 36.3 jit_solution(10612699660614001787)
XLA Ops:
  0.6 1.8 %send.1 = (bf16[32,56,128]{2,1,0:T(8,128)(2,1)S(1)}, f32[16,24,384]{2,1,0:T(8,128)S(1)}, bf16[1328,256]{1,0:T(8,128)(2,1)S(1)}) custom-call(bf16[12,12288]{1,0:T(8,128)(2,1)} %coef_hbm.1, s32[3,768]{1,0:T(4,128)} %exp_hbm.1, bf16[384,384]{1,0:T(8,128)(2,1)} %constant.7.clone.spread_hbm, bf16[384,256]{1,0:T(8,128)(2,1)} %constant.8.clone.edge_hbm, ...), custom_call_target="tpu_custom_call" | custom-call | tf_op jit(solution)/shard_map/send/pallas_call | solution.py:293
  2.4 22.0 %all_to_all.10.got_ref = bf16[32,56,128]{2,1,0:T(8,128)(2,1)S(1)} all-to-all(bf16[32,56,128]{2,1,0:T(8,128)(2,1)S(1)} %get-tuple-element.9), channel_id=1, replica_groups=mesh['px'=4,'py'=8] {'px','py'}, dimensions={0} | all-to-all | bytes 917504 | tf_op jit(solution)/shard_map/all_to_all | solution.py:20
  24.4 2.1 %receive.1 = (f32[16,24,384]{2,1,0:T(8,128)}, f32[16,24,384]{2,1,0:T(8,128)}, f32[32,1,128]{2,1,0:T(1,128)S(1)}) custom-call(bf16[32,56,128]{2,1,0:T(8,128)(2,1)S(1)} %all_to_all.10.got_ref, f32[16,24,384]{2,1,0:T(8,128)S(1)} %get-tuple-element.10.right_ref, bf16[1328,256]{1,0:T(8,128)(2,1)S(1)} %get-tuple-element.11.table_ref), custom_call_target="tpu_custom_call" | custom-call | tf_op jit(solution)/shard_map/receive/pallas_call | solution.py:321
  26.4 9.3 %all_to_all.11.parts_ref = f32[32,1,128]{2,1,0:T(1,128)S(1)} all-to-all(f32[32,1,128]{2,1,0:T(1,128)S(1)} %get-tuple-element.14), channel_id=1, replica_groups=mesh['px'=4,'py'=8] {'px','py'}, dimensions={0} | all-to-all | bytes 32768 | tf_op jit(solution)/shard_map/all_to_all | solution.py:20
  35.7 0.6 %finish.1 = f32[1,1]{1,0:T(1,128)} custom-call(f32[32,1,128]{2,1,0:T(1,128)S(1)} %all_to_all.11.parts_ref), custom_call_target="tpu_custom_call" | custom-call | tf_op jit(solution)/shard_map/finish/pallas_call | solution.py:342

commit v4 on v3

--- a/solution.py
+++ b/solution.py
@@ -10,7 +10,7 @@
 
 AXES = ("px", "py")
 LANES = 128
-ROWS = 56
+ROWS = 52
 TAIL = 48
 LAYERS = 12
 GROUP = 4
@@ -46,15 +46,6 @@
     y_high, y_low = full[:, :, cy - 1], full[:, :, 0]
     table = np.concatenate([x_high, x_low, y_high, y_low, x_high, x_low], axis=1)
     return np.concatenate(halves(table), axis=1)
-
-
-def spread_table(cx, cy, per):
-    quarter = cy // 4
-    blocks = cx // 4 * quarter
-    cell = np.arange(cx * cy)
-    block = cell // cy // 4 * quarter + cell % cy // 4
-    same = (np.arange(per * blocks) % blocks)[:, None] == block[None, :]
-    return same.astype(jnp.bfloat16)
 
 
 def depth_table():
@@ -94,24 +85,30 @@
     return table.astype(jnp.bfloat16)
 
 
+def spread_table(cx, cy):
+    blocks, patch = cx * cy // 16, cx * cy
+    own = lax.broadcasted_iota(jnp.int32, (patch, patch), 0) % blocks
+    cell = lax.broadcasted_iota(jnp.int32, (1, patch), 1)
+    block = cell // (4 * cy) * (cy // 4) + cell % cy // 4
+    return jnp.where(own == block, 1.0, 0.0).astype(jnp.bfloat16)
+
+
 def send_kernel(
-    count_x, count_y, cx, cy, coef_hbm, exp_hbm, spread_hbm, edge_hbm, right_hbm, table_hbm,
-    out_ref, right_ref, table_ref, coef_ref, exp_ref, spread_ref, edge_ref, factor, scaled, edge, sems,
+    count_x, count_y, cx, cy, coef_hbm, exp_hbm, edge_hbm, right_hbm, table_hbm,
+    out_ref, right_ref, table_ref, coef_ref, exp_ref, edge_ref, factor, scaled, edge, sems,
 ):
-    pairs = [
-        (exp_hbm, exp_ref), (spread_hbm, spread_ref), (coef_hbm, coef_ref), (edge_hbm, edge_ref),
-        (right_hbm, right_ref), (table_hbm, table_ref),
-    ]
+    pairs = [(exp_hbm, exp_ref), (coef_hbm, coef_ref), (edge_hbm, edge_ref)]
+    pairs += [(right_hbm, right_ref), (table_hbm, table_ref)]
     loads = [pltpu.make_async_copy(a, b, sems.at[n]) for n, (a, b) in enumerate(pairs)]
     for load in loads:
         load.start()
-    loads[0].wait()
-    loads[1].wait()
     peers = count_x * count_y
     patch = cx * cy
     blocks = patch // 16
     per = patch // blocks
     edges = 2 * cy + 2 * cx
+    spread = spread_table(cx, cy)
+    loads[0].wait()
     power = lax.shift_left(jnp.int32(1), exp_ref[...] + 15).astype(jnp.float32) * (2.0**-15)
     lane = lax.broadcasted_iota(jnp.int32, (per, patch), 1)
     row = lax.broadcasted_iota(jnp.int32, (per, patch), 0)
@@ -123,58 +120,70 @@
         ]
         left = jnp.concatenate(stacked, axis=0).astype(jnp.bfloat16)
         factor[h * 3 * per : (h + 1) * 3 * per, :] = jnp.dot(
-            left, spread_ref[...], preferred_element_type=jnp.float32
+            left, spread, preferred_element_type=jnp.float32
         )
     layer = lax.broadcasted_iota(jnp.int32, (LAYERS, patch), 0)
-    loads[2].wait()
-    for p in range(peers):
-        base = p // per * 3 * per + p % per
-        rows = [
-            jnp.broadcast_to(factor[base + b * per : base + b * per + 1, :], (LAYERS, patch))
-            for b in range(3)
-        ]
-        spread = jnp.where(layer < 4, rows[0], jnp.where(layer < 8, rows[1], rows[2]))
-        part = coef_ref[:, p * patch : (p + 1) * patch].astype(jnp.float32) * spread
-        part = part.astype(jnp.bfloat16)
-        scaled[p, 0:LAYERS, :] = part
-        for t in range(3):
-            out_ref[p, 16 * t : 16 * t + LAYERS, :] = part[:, t * LANES : (t + 1) * LANES]
-    loads[3].wait()
-    found = jnp.dot(
-        scaled[...].reshape(peers * 16, patch), edge_ref[...], preferred_element_type=jnp.float32
-    )
-    edge[...] = (found[:, :LANES] + found[:, LANES:]).reshape(peers, 16, LANES)
+    wide = lax.broadcasted_iota(jnp.int32, (4, LANES), 1)
     lane = lax.broadcasted_iota(jnp.int32, (16, LANES), 1)
     from_left = (lane < cy) | ((lane >= edges) & (lane < edges + cy))
     from_right = ((lane >= cy) & (lane < 2 * cy)) | (lane >= edges + cy)
     from_below = (lane >= 2 * cy) & (lane < 2 * cy + cx)
     nothing = jnp.zeros((16, LANES), jnp.float32)
-    for p in range(peers):
-        i, j = divmod(p, count_y)
-        left = edge[p - count_y] if i > 0 else nothing
-        right = edge[p + count_y] if i < count_x - 1 else nothing
-        below = edge[p - 1] if j > 0 else nothing
-        above = edge[p + 1] if j < count_y - 1 else nothing
-        value = jnp.where(
-            from_left, left, jnp.where(from_right, right, jnp.where(from_below, below, above))
+
+    def scale_row(i):
+        for p in range(i * count_y, (i + 1) * count_y):
+            base = p // per * 3 * per + p % per
+            rows = [
+                jnp.broadcast_to(factor[base + b * per : base + b * per + 1, :], (LAYERS, patch))
+                for b in range(3)
+            ]
+            scale = jnp.where(layer < 4, rows[0], jnp.where(layer < 8, rows[1], rows[2]))
+            part = coef_ref[:, p * patch : (p + 1) * patch].astype(jnp.float32) * scale
+            part = part.astype(jnp.bfloat16)
+            scaled[p, 0:LAYERS, :] = part
+            for t in range(3):
+                tile = part[:, t * LANES : (t + 1) * LANES]
+                for k in range(3):
+                    out_ref[p, 4 * t + k] = tile[4 * k : 4 * k + 4]
+        row = pl.ds(i * count_y, count_y)
+        found = jnp.dot(
+            scaled[row].reshape(count_y * 16, patch),
+            edge_ref[...],
+            preferred_element_type=jnp.float32,
         )
-        high = value.astype(jnp.bfloat16).astype(jnp.float32)
-        low = value - high
-        tile = jnp.where(lane < edges, high, low)
-        for t in range(3):
-            out_ref[p, 16 * t + LAYERS : 16 * t + 16, :] = tile[4 * t : 4 * t + 4].astype(
-                jnp.bfloat16
+        edge[row] = (found[:, :LANES] + found[:, LANES:]).reshape(count_y, 16, LANES)
+
+    def join_row(i):
+        for p in range(i * count_y, (i + 1) * count_y):
+            j = p % count_y
+            left = edge[p - count_y] if i > 0 else nothing
+            right = edge[p + count_y] if i < count_x - 1 else nothing
+            below = edge[p - 1] if j > 0 else nothing
+            above = edge[p + 1] if j < count_y - 1 else nothing
+            value = jnp.where(
+                from_left, left, jnp.where(from_right, right, jnp.where(from_below, below, above))
             )
-        wide = lane[:4]
-        first = pltpu.roll(low[0:8], LANES - 2 * cy, 1)[0:4]
-        second = pltpu.roll(low[0:8], LANES - 2 * cy + 2 * cx, 1)[4:8]
-        third = pltpu.roll(low[8:16], (4 * cx - 2 * cy) % LANES, 1)[0:4]
-        tail = jnp.where(wide < 2 * cx, first, jnp.where(wide < 4 * cx, second, third))
-        tail = jnp.where(wide < 6 * cx, tail, 0.0)
-        tail = jnp.concatenate([tail, jnp.zeros((4, LANES), jnp.float32)], axis=0)
-        out_ref[p, TAIL:ROWS, :] = tail.astype(jnp.bfloat16)
+            high = value.astype(jnp.bfloat16).astype(jnp.float32)
+            low = value - high
+            tile = jnp.where(lane < edges, high, low).astype(jnp.bfloat16)
+            for t in range(3):
+                out_ref[p, 4 * t + 3] = tile[4 * t : 4 * t + 4]
+            first = pltpu.roll(low[0:8], LANES - 2 * cy, 1)[0:4]
+            second = pltpu.roll(low[0:8], LANES - 2 * cy + 2 * cx, 1)[4:8]
+            third = pltpu.roll(low[8:16], (4 * cx - 2 * cy) % LANES, 1)[0:4]
+            tail = jnp.where(wide < 2 * cx, first, jnp.where(wide < 4 * cx, second, third))
+            tail = jnp.where(wide < 6 * cx, tail, 0.0)
+            out_ref[p, TAIL // 4] = tail.astype(jnp.bfloat16)
+
+    loads[1].wait()
+    loads[2].wait()
+    for i in range(count_x):
+        scale_row(i)
+        if i > 0:
+            join_row(i - 1)
+    join_row(count_x - 1)
+    loads[3].wait()
     loads[4].wait()
-    loads[5].wait()
 
 
 def receive_table(cx, cy):
@@ -281,29 +290,27 @@
     peers = count_x * count_y
     cx, cy, depth = right_side.shape
     patch = cx * cy
-    per = 16
     vmem = pl.BlockSpec(memory_space=pltpu.VMEM)
     hbm = pl.BlockSpec(memory_space=pltpu.HBM)
     tables = jnp.asarray(receive_table(cx, cy))
     kept = [(right_side.shape, right_side.dtype), (tables.shape, tables.dtype)]
-    kept = [((peers, ROWS, LANES), jnp.bfloat16)] + kept
+    kept = [((peers, ROWS // 4, 4, LANES), jnp.bfloat16)] + kept
     held = sum(int(np.prod(shape)) * jnp.dtype(dtype).itemsize for shape, dtype in kept)
     near = held <= 2 << 20
     place = pltpu.VMEM if near else jax.ShapeDtypeStruct
     messages, right_side, tables = pl.pallas_call(
         functools.partial(send_kernel, count_x, count_y, cx, cy),
         out_shape=[place(*k) for k in kept],
-        in_specs=[hbm] * 6,
+        in_specs=[hbm] * 5,
         out_specs=[vmem] * 3,
         scratch_shapes=[
             pltpu.VMEM(coefficients.shape, coefficients.dtype),
             pltpu.VMEM(exponents.shape, exponents.dtype),
-            pltpu.VMEM((patch, patch), jnp.bfloat16),
             pltpu.VMEM((patch, 2 * LANES), jnp.bfloat16),
             pltpu.VMEM((peers * 3, patch), jnp.float32),
             pltpu.VMEM((peers, 16, patch), jnp.bfloat16),
             pltpu.VMEM((peers, 16, LANES), jnp.float32),
-            pltpu.SemaphoreType.DMA((6,)),
+            pltpu.SemaphoreType.DMA((5,)),
         ],
         compiler_params=pltpu.CompilerParams(
             vmem_limit_bytes=(64 << 20) - held - (256 << 10) if near else 48 << 20
@@ -312,7 +319,6 @@
     )(
         coefficients,
         exponents,
-        jnp.asarray(spread_table(cx, cy, per)),
         jnp.asarray(edge_table(cx, cy)),
         right_side,
         tables,

time: 36.6 us -> 35.7 us (0.975)
  blocking collectives: 31.2 us -> 30.5 us
    all_to_all x2, blocking collectives: 31.2 us -> 30.5 us  [exchange(): return lax.all_to_all(array, AXES, split_axis=0, concat_axis=0, tiled=True)]
where the time goes in v4:
time: 35.7 us; the launch traced here: 35.5 us
  blocking collectives  30.5 us (85%)
  Pallas kernels  4.28 us (12%)
  between operations  0.65 us (2%)
    all_to_all x2, blocking collectives, exchange(): return lax.all_to_all(array, AXES, split_axis=0, concat_axis=0, tiled=True)  30.5 us
    pallas_call x1, Pallas kernels, shards(): pl.pallas_call(functools.partial(receive_kernel, cx, cy), out_shape=(jax....  2.08 us
    pallas_call x1, Pallas kernels, shards(): pl.pallas_call(functools.partial(send_kernel, count_x, count_y, cx, cy),...  1.59 us

profile of v4, /device:TPU:0, one launch (start us, length us, event | category | flops | bytes accessed | tf_op | source)
XLA Modules:
  0.0 35.5 jit_solution(3396786782980517690)
XLA Ops:
  0.6 1.6 %send.1 = (bf16[32,13,4,128]{3,2,1,0:T(4,128)(2,1)S(1)}, f32[16,24,384]{2,1,0:T(8,128)S(1)}, bf16[1328,256]{1,0:T(8,128)(2,1)S(1)}) custom-call(bf16[12,12288]{1,0:T(8,128)(2,1)} %coef_hbm.1, s32[3,768]{1,0:T(4,128)} %exp_hbm.1, bf16[384,256]{1,0:T(8,128)(2,1)} %constant.5.clone.edge_hbm, f32[16,24,384]{2,1,0:T(8,128)} %right_hbm.1, ...), custom_call_target="tpu_custom_call" | custom-call | tf_op jit(solution)/shard_map/send/pallas_call | solution.py:301
  2.2 21.3 %all_to_all.10.got_ref = bf16[32,13,4,128]{3,2,1,0:T(4,128)(2,1)S(1)} all-to-all(bf16[32,13,4,128]{3,2,1,0:T(4,128)(2,1)S(1)} %get-tuple-element.9), channel_id=1, replica_groups=mesh['px'=4,'py'=8] {'px','py'}, dimensions={0} | all-to-all | bytes 851968 | tf_op jit(solution)/shard_map/all_to_all | solution.py:20
  23.5 2.1 %receive.1 = (f32[16,24,384]{2,1,0:T(8,128)}, f32[16,24,384]{2,1,0:T(8,128)}, f32[32,1,128]{2,1,0:T(1,128)S(1)}) custom-call(bf16[32,13,4,128]{3,2,1,0:T(4,128)(2,1)S(1)} %all_to_all.10.got_ref, f32[16,24,384]{2,1,0:T(8,128)S(1)} %get-tuple-element.10.right_ref, bf16[1328,256]{1,0:T(8,128)(2,1)S(1)} %get-tuple-element.11.table_ref), custom_call_target="tpu_custom_call" | custom-call | tf_op jit(solution)/shard_map/receive/pallas_call | solution.py:327
  25.6 9.3 %all_to_all.11.parts_ref = f32[32,1,128]{2,1,0:T(1,128)S(1)} all-to-all(f32[32,1,128]{2,1,0:T(1,128)S(1)} %get-tuple-element.14), channel_id=1, replica_groups=mesh['px'=4,'py'=8] {'px','py'}, dimensions={0} | all-to-all | bytes 32768 | tf_op jit(solution)/shard_map/all_to_all | solution.py:20
  34.9 0.6 %finish.1 = f32[1,1]{1,0:T(1,128)} custom-call(f32[32,1,128]{2,1,0:T(1,128)S(1)} %all_to_all.11.parts_ref), custom_call_target="tpu_custom_call" | custom-call | tf_op jit(solution)/shard_map/finish/pallas_call | solution.py:348

commit v5 on v4

--- a/solution.py
+++ b/solution.py
@@ -14,10 +14,20 @@
 TAIL = 48
 LAYERS = 12
 GROUP = 4
-
-
-def exchange(array):
-    return lax.all_to_all(array, AXES, split_axis=0, concat_axis=0, tiled=True)
+SEQUENCE = (7, 4, 3, 2, 5, 6, 1, 0)
+WITHIN = (1, 3, 0, 2)
+
+
+def order_of(count_x, count_y):
+    groups = count_x * count_y // GROUP
+    order = SEQUENCE if groups == len(SEQUENCE) else range(groups)
+    return [GROUP * g + d for g in order for d in WITHIN]
+
+
+def exchange(array, order):
+    return lax.all_to_all(
+        array, AXES, split_axis=0, concat_axis=0, tiled=True, axis_index_groups=[order]
+    )
 
 
 def basis4():
@@ -48,7 +58,8 @@
     return np.concatenate(halves(table), axis=1)
 
 
-def depth_table():
+def depth_table(order):
+    at = np.argsort([d % GROUP for d in order[:GROUP]])
     basis = basis4()
     table = np.zeros((5, GROUP, LAYERS, GROUP, ROWS))
     for s in range(GROUP):
@@ -57,9 +68,9 @@
             for a in range(4):
                 layer = 4 * block + a
                 for t in range(3):
-                    table[t, s, point, s, 16 * t + layer] = basis[a, k]
-                table[3, s, point, s, 16 * block + 12 + a] = basis[a, k]
-                table[4, s, point, s, TAIL + a] = basis[a, k]
+                    table[t, s, point, at[s], 16 * t + layer] = basis[a, k]
+                table[3, s, point, at[s], 16 * block + 12 + a] = basis[a, k]
+                table[4, s, point, at[s], TAIL + a] = basis[a, k]
     return np.concatenate(halves(table.reshape(5 * GROUP * LAYERS, GROUP * ROWS)), axis=0)
 
 
@@ -94,7 +105,7 @@
 
 
 def send_kernel(
-    count_x, count_y, cx, cy, coef_hbm, exp_hbm, edge_hbm, right_hbm, table_hbm,
+    order, count_x, count_y, cx, cy, coef_hbm, exp_hbm, edge_hbm, right_hbm, table_hbm,
     out_ref, right_ref, table_ref, coef_ref, exp_ref, edge_ref, factor, scaled, edge, sems,
 ):
     pairs = [(exp_hbm, exp_ref), (coef_hbm, coef_ref), (edge_hbm, edge_ref)]
@@ -103,6 +114,7 @@
     for load in loads:
         load.start()
     peers = count_x * count_y
+    place = np.argsort(order)
     patch = cx * cy
     blocks = patch // 16
     per = patch // blocks
@@ -130,21 +142,23 @@
     from_below = (lane >= 2 * cy) & (lane < 2 * cy + cx)
     nothing = jnp.zeros((16, LANES), jnp.float32)
 
+    for p in range(peers):
+        base = p // per * 3 * per + p % per
+        rows = [
+            jnp.broadcast_to(factor[base + b * per : base + b * per + 1, :], (LAYERS, patch))
+            for b in range(3)
+        ]
+        scale = jnp.where(layer < 4, rows[0], jnp.where(layer < 8, rows[1], rows[2]))
+        scaled[p, 0:LAYERS, :] = scale.astype(jnp.bfloat16)
+
     def scale_row(i):
         for p in range(i * count_y, (i + 1) * count_y):
-            base = p // per * 3 * per + p % per
-            rows = [
-                jnp.broadcast_to(factor[base + b * per : base + b * per + 1, :], (LAYERS, patch))
-                for b in range(3)
-            ]
-            scale = jnp.where(layer < 4, rows[0], jnp.where(layer < 8, rows[1], rows[2]))
-            part = coef_ref[:, p * patch : (p + 1) * patch].astype(jnp.float32) * scale
-            part = part.astype(jnp.bfloat16)
+            part = coef_ref[:, p * patch : (p + 1) * patch] * scaled[p, 0:LAYERS, :]
             scaled[p, 0:LAYERS, :] = part
             for t in range(3):
                 tile = part[:, t * LANES : (t + 1) * LANES]
                 for k in range(3):
-                    out_ref[p, 4 * t + k] = tile[4 * k : 4 * k + 4]
+                    out_ref[place[p], 4 * t + k] = tile[4 * k : 4 * k + 4]
         row = pl.ds(i * count_y, count_y)
         found = jnp.dot(
             scaled[row].reshape(count_y * 16, patch),
@@ -167,13 +181,13 @@
             low = value - high
             tile = jnp.where(lane < edges, high, low).astype(jnp.bfloat16)
             for t in range(3):
-                out_ref[p, 4 * t + 3] = tile[4 * t : 4 * t + 4]
+                out_ref[place[p], 4 * t + 3] = tile[4 * t : 4 * t + 4]
             first = pltpu.roll(low[0:8], LANES - 2 * cy, 1)[0:4]
             second = pltpu.roll(low[0:8], LANES - 2 * cy + 2 * cx, 1)[4:8]
             third = pltpu.roll(low[8:16], (4 * cx - 2 * cy) % LANES, 1)[0:4]
             tail = jnp.where(wide < 2 * cx, first, jnp.where(wide < 4 * cx, second, third))
             tail = jnp.where(wide < 6 * cx, tail, 0.0)
-            out_ref[p, TAIL // 4] = tail.astype(jnp.bfloat16)
+            out_ref[place[p], TAIL // 4] = tail.astype(jnp.bfloat16)
 
     loads[1].wait()
     loads[2].wait()
@@ -186,8 +200,8 @@
     loads[4].wait()
 
 
-def receive_table(cx, cy):
-    depth = depth_table()
+def receive_table(order, cx, cy):
+    depth = depth_table(order)
     depth = np.pad(depth, ((0, 0), (0, 2 * LANES - depth.shape[1])))
     planes = plane_windows(cx, cy).reshape(-1, 2 * LANES)
     return np.concatenate([depth, planes, pick_table(cx, cy)], axis=0)
@@ -199,10 +213,11 @@
 
 
 def receive_kernel(
-    cx, cy, got_ref, right_ref, table_ref, dec_hbm, res_hbm, sum_ref,
+    order, cx, cy, got_ref, right_ref, table_ref, dec_hbm, res_hbm, sum_ref,
     high_ref, low_ref, edge_ref, dec_ref, res_ref, sems,
 ):
     peers = got_ref.shape[0]
+    groups = np.argsort([d // GROUP for d in order[::GROUP]])
     depth = peers * LAYERS
     patch = cx * cy
     count = GROUP * LAYERS
@@ -218,7 +233,8 @@
     in_block = (lane >= block * third) & (lane < (block + 1) * third)
     for g in range(0, peers // GROUP, 2):
         messages = [
-            got_ref[GROUP * h : GROUP * (h + 1)].reshape(GROUP * ROWS, LANES) for h in (g, g + 1)
+            got_ref[GROUP * h : GROUP * (h + 1)].reshape(GROUP * ROWS, LANES)
+            for h in (groups[g], groups[g + 1])
         ]
         both = jnp.dot(
             table_ref[:tables, : GROUP * ROWS], jnp.concatenate(messages, axis=1), preferred_element_type=jnp.float32
@@ -292,14 +308,15 @@
     patch = cx * cy
     vmem = pl.BlockSpec(memory_space=pltpu.VMEM)
     hbm = pl.BlockSpec(memory_space=pltpu.HBM)
-    tables = jnp.asarray(receive_table(cx, cy))
+    order = order_of(count_x, count_y)
+    tables = jnp.asarray(receive_table(order, cx, cy))
     kept = [(right_side.shape, right_side.dtype), (tables.shape, tables.dtype)]
     kept = [((peers, ROWS // 4, 4, LANES), jnp.bfloat16)] + kept
     held = sum(int(np.prod(shape)) * jnp.dtype(dtype).itemsize for shape, dtype in kept)
     near = held <= 2 << 20
     place = pltpu.VMEM if near else jax.ShapeDtypeStruct
     messages, right_side, tables = pl.pallas_call(
-        functools.partial(send_kernel, count_x, count_y, cx, cy),
+        functools.partial(send_kernel, order, count_x, count_y, cx, cy),
         out_shape=[place(*k) for k in kept],
         in_specs=[hbm] * 5,
         out_specs=[vmem] * 3,
@@ -323,9 +340,9 @@
         right_side,
         tables,
     )
-    got = exchange(messages)
+    got = exchange(messages, order)
     decoded, residual, parts = pl.pallas_call(
-        functools.partial(receive_kernel, cx, cy),
+        functools.partial(receive_kernel, order, cx, cy),
         out_shape=(
             jax.ShapeDtypeStruct((cx, cy, depth), jnp.float32),
             jax.ShapeDtypeStruct((cx, cy, depth), jnp.float32),
@@ -344,7 +361,7 @@
         compiler_params=pltpu.CompilerParams(vmem_limit_bytes=(12 << 20) * peers // 32),
         name="receive",
     )(got, right_side, tables)
-    parts = exchange(parts)
+    parts = exchange(parts, order)
     rms = pl.pallas_call(
         functools.partial(finish_kernel, patch * depth * peers),
         out_shape=jax.ShapeDtypeStruct((1, 1), jnp.float32),

time: 35.7 us -> 35 us (0.980)
  blocking collectives: 30.5 us -> 29.8 us
    all_to_all x2, blocking collectives: 30.5 us -> 29.8 us  [exchange(): lax.all_to_all(array, AXES, split_axis=0, concat_axis=0, tiled=True, axis...]
where the time goes in v5:
time: 35 us; the launch traced here: 34.8 us
  blocking collectives  29.8 us (85%)
  Pallas kernels  4.28 us (12%)
  between operations  0.65 us (2%)
    all_to_all x2, blocking collectives, exchange(): lax.all_to_all(array, AXES, split_axis=0, concat_axis=0, tiled=True, axis...  29.8 us
    pallas_call x1, Pallas kernels, shards(): pl.pallas_call(functools.partial(receive_kernel, order, cx, cy), out_shap...  2.09 us
    pallas_call x1, Pallas kernels, shards(): pl.pallas_call(functools.partial(send_kernel, order, count_x, count_y, cx...  1.57 us

profile of v5, /device:TPU:0, one launch (start us, length us, event | category | flops | bytes accessed | tf_op | source)
XLA Modules:
  0.0 34.8 jit_solution(12557937570130403217)
XLA Ops:
  0.6 1.6 %send.1 = (bf16[32,13,4,128]{3,2,1,0:T(4,128)(2,1)S(1)}, f32[16,24,384]{2,1,0:T(8,128)S(1)}, bf16[1328,256]{1,0:T(8,128)(2,1)S(1)}) custom-call(bf16[12,12288]{1,0:T(8,128)(2,1)} %coef_hbm.1, s32[3,768]{1,0:T(4,128)} %exp_hbm.1, bf16[384,256]{1,0:T(8,128)(2,1)} %constant.5.clone.edge_hbm, f32[16,24,384]{2,1,0:T(8,128)} %right_hbm.1, ...), custom_call_target="tpu_custom_call" | custom-call | tf_op jit(solution)/shard_map/send/pallas_call | solution.py:318
  2.2 20.3 %all_to_all.10.got_ref = bf16[32,13,4,128]{3,2,1,0:T(4,128)(2,1)S(1)} all-to-all(bf16[32,13,4,128]{3,2,1,0:T(4,128)(2,1)S(1)} %get-tuple-element.9), channel_id=1, replica_groups={{29,31,28,30,17,19,16,18,13,15,12,14,9,11,8,10,21,23,20,22,25,27,24,26,..., dimensions={0} | all-to-all | bytes 851968 | tf_op jit(solution)/shard_map/all_to_all | solution.py:28
  22.5 2.1 %receive.1 = (f32[16,24,384]{2,1,0:T(8,128)}, f32[16,24,384]{2,1,0:T(8,128)}, f32[32,1,128]{2,1,0:T(1,128)S(1)}) custom-call(bf16[32,13,4,128]{3,2,1,0:T(4,128)(2,1)S(1)} %all_to_all.10.got_ref, f32[16,24,384]{2,1,0:T(8,128)S(1)} %get-tuple-element.10.right_ref, bf16[1328,256]{1,0:T(8,128)(2,1)S(1)} %get-tuple-element.11.table_ref), custom_call_target="tpu_custom_call" | custom-call | tf_op jit(solution)/shard_map/receive/pallas_call | solution.py:344
  24.6 9.6 %all_to_all.11.parts_ref = f32[32,1,128]{2,1,0:T(1,128)S(1)} all-to-all(f32[32,1,128]{2,1,0:T(1,128)S(1)} %get-tuple-element.14), channel_id=1, replica_groups={{29,31,28,30,17,19,16,18,13,15,12,14,9,11,8,10,21,23,20,22,25,27,24,26,..., dimensions={0} | all-to-all | bytes 32768 | tf_op jit(solution)/shard_map/all_to_all | solution.py:28
  34.1 0.6 %finish.1 = f32[1,1]{1,0:T(1,128)} custom-call(f32[32,1,128]{2,1,0:T(1,128)S(1)} %all_to_all.11.parts_ref), custom_call_target="tpu_custom_call" | custom-call | tf_op jit(solution)/shard_map/finish/pallas_call | solution.py:365

commit v6 on v5

--- a/solution.py
+++ b/solution.py
@@ -71,7 +71,9 @@
                     table[t, s, point, at[s], 16 * t + layer] = basis[a, k]
                 table[3, s, point, at[s], 16 * block + 12 + a] = basis[a, k]
                 table[4, s, point, at[s], TAIL + a] = basis[a, k]
-    return np.concatenate(halves(table.reshape(5 * GROUP * LAYERS, GROUP * ROWS)), axis=0)
+    table = np.concatenate(halves(table.reshape(5 * GROUP * LAYERS, GROUP * ROWS)), axis=1)
+    table = np.pad(table, ((0, 0), (0, 4 * LANES - table.shape[1])))
+    return np.stack([table[:, : 2 * LANES], table[:, 2 * LANES :]])
 
 
 def plane_windows(cx, cy):
@@ -201,10 +203,8 @@
 
 
 def receive_table(order, cx, cy):
-    depth = depth_table(order)
-    depth = np.pad(depth, ((0, 0), (0, 2 * LANES - depth.shape[1])))
-    planes = plane_windows(cx, cy).reshape(-1, 2 * LANES)
-    return np.concatenate([depth, planes, pick_table(cx, cy)], axis=0)
+    parts = [depth_table(order), plane_windows(cx, cy), pick_table(cx, cy)]
+    return np.concatenate([part.reshape(-1, 2 * LANES) for part in parts], axis=0)
 
 
 def split(value):
@@ -221,25 +221,27 @@
     depth = peers * LAYERS
     patch = cx * cy
     count = GROUP * LAYERS
-    contract = (((1,), (1,)), ((), ()))
+    half = patch // 2
+    starts = [0, 5 * count, 10 * count] + [10 * count + half * n for n in range(1, 5)]
+    starts = starts + [table_ref.shape[0]]
+    table = [table_ref[a:b] for a, b in zip(starts[:-1], starts[1:])]
+    deep = jnp.concatenate(table[:2], axis=1)[:, : 2 * GROUP * ROWS]
     row = lax.broadcasted_iota(jnp.int32, (count, LANES), 0)
     lane = lax.broadcasted_iota(jnp.int32, (count, LANES), 1)
     third = 2 * cx
-    half = patch // 2
-    tables = 10 * count
-    flat = [table_ref[tables + half * n : tables + half * (n + 1)] for n in range(4)]
-    pick = table_ref[tables + 4 * half :]
     block = row // 4 % 3
     in_block = (lane >= block * third) & (lane < (block + 1) * third)
     for g in range(0, peers // GROUP, 2):
-        messages = [
-            got_ref[GROUP * h : GROUP * (h + 1)].reshape(GROUP * ROWS, LANES)
-            for h in (groups[g], groups[g + 1])
-        ]
+        both = jnp.concatenate(
+            [
+                got_ref[GROUP * h : GROUP * (h + 1)].reshape(GROUP * ROWS, LANES)
+                for h in (groups[g], groups[g + 1])
+            ],
+            axis=1,
+        )
         both = jnp.dot(
-            table_ref[:tables, : GROUP * ROWS], jnp.concatenate(messages, axis=1), preferred_element_type=jnp.float32
-        )
-        both = both[: 5 * count] + both[5 * count :]
+            deep, jnp.concatenate([both, both], axis=0), preferred_element_type=jnp.float32
+        )
         for h in range(2):
             at = (g + h) * count
             for t in range(5):
@@ -250,25 +252,31 @@
                 high_ref[at : at + count, t * LANES : (t + 1) * LANES] = high
                 low_ref[at : at + count, t * LANES : (t + 1) * LANES] = low
 
-    def across(table, ref, start):
+    def across(tables, refs, start):
         return lax.dot_general(
-            table, ref[:, start : start + 2 * LANES], contract, preferred_element_type=jnp.float32
-        )
-
+            jnp.concatenate(tables, axis=1),
+            jnp.concatenate([ref[:, start : start + 2 * LANES] for ref in refs], axis=1),
+            (((1,), (1,)), ((), ())),
+            preferred_element_type=jnp.float32,
+        )
+
+    row = lax.broadcasted_iota(jnp.int32, (cy, depth), 0)
+    lane = lax.broadcasted_iota(jnp.int32, (cy, depth), 1)
     stores = []
-    for w, start in enumerate((0, patch - 2 * LANES)):
-        found = across(flat[w], high_ref, start) + across(flat[w], low_ref, start)
-        found = found + across(flat[2 + w], high_ref, start)
+
+    def store(source, target):
+        stores.append(pltpu.make_async_copy(source, target, sems.at[len(stores)]))
+        stores[-1].start()
+
+    def decode(w, start):
+        found = across(
+            [table[2 + w], table[2 + w], table[4 + w]], [high_ref, low_ref, high_ref], start
+        )
         part = pl.ds(w * cx // 2, cx // 2)
         dec_ref[part] = found.reshape(cx // 2, cy, depth)
-        stores.append(pltpu.make_async_copy(dec_ref.at[part], dec_hbm.at[part], sems.at[w]))
-        stores[-1].start()
-    edge_ref[...] = across(pick, high_ref, patch) + across(pick, low_ref, patch)
-
-    row = lax.broadcasted_iota(jnp.int32, (cy, depth), 0)
-    lane = lax.broadcasted_iota(jnp.int32, (cy, depth), 1)
-    total = jnp.zeros((8, LANES), jnp.float32)
-    for x in range(cx):
+        store(dec_ref.at[part], dec_hbm.at[part])
+
+    def finish(x, total):
         here = dec_ref[x]
         beside = dec_ref[x - 1] if x > 0 else edge_ref[0:cy]
         beside = beside + (dec_ref[x + 1] if x < cx - 1 else edge_ref[cy : 2 * cy])
@@ -286,14 +294,21 @@
                 total = total + square[r : r + 8, c : c + LANES]
         if x % 4 == 3:
             part = pl.ds(x - 3, 4)
-            stores.append(
-                pltpu.make_async_copy(res_ref.at[part], res_hbm.at[part], sems.at[2 + x // 4])
-            )
-            stores[-1].start()
+            store(res_ref.at[part], res_hbm.at[part])
+        return total
+
+    total = jnp.zeros((8, LANES), jnp.float32)
+    decode(0, 0)
+    edge_ref[...] = across([table[6], table[6]], [high_ref, low_ref], patch)
+    for x in range(cx // 2 - 1):
+        total = finish(x, total)
+    decode(1, patch - 2 * LANES)
+    for x in range(cx // 2 - 1, cx):
+        total = finish(x, total)
     total = jnp.sum(total, axis=0, keepdims=True)
     sum_ref[...] = jnp.broadcast_to(total[None], sum_ref.shape)
-    for store in stores:
-        store.wait()
+    for copy in stores:
+        copy.wait()
 
 
 def finish_kernel(cells, parts_ref, rms_ref):

time: 35 us -> 34.9 us (level)
  no operation moved by 1% of the time
where the time goes in v6:
time: 34.9 us; the launch traced here: 34.7 us
  blocking collectives  29.8 us (85%)
  Pallas kernels  4.19 us (12%)
  between operations  0.65 us (2%)
    all_to_all x2, blocking collectives, exchange(): lax.all_to_all(array, AXES, split_axis=0, concat_axis=0, tiled=True, axis...  29.8 us
    pallas_call x1, Pallas kernels, shards(): pl.pallas_call(functools.partial(receive_kernel, order, cx, cy), out_shap...  2 us
    pallas_call x1, Pallas kernels, shards(): pl.pallas_call(functools.partial(send_kernel, order, count_x, count_y, cx...  1.57 us

profile of v6, /device:TPU:0, one launch (start us, length us, event | category | flops | bytes accessed | tf_op | source)
XLA Modules:
  0.0 34.7 jit_solution(13238256192591675462)
XLA Ops:
  0.6 1.6 %send.1 = (bf16[32,13,4,128]{3,2,1,0:T(4,128)(2,1)S(1)}, f32[16,24,384]{2,1,0:T(8,128)S(1)}, bf16[1328,256]{1,0:T(8,128)(2,1)S(1)}) custom-call(bf16[12,12288]{1,0:T(8,128)(2,1)} %coef_hbm.1, s32[3,768]{1,0:T(4,128)} %exp_hbm.1, bf16[384,256]{1,0:T(8,128)(2,1)} %constant.5.clone.edge_hbm, f32[16,24,384]{2,1,0:T(8,128)} %right_hbm.1, ...), custom_call_target="tpu_custom_call" | custom-call | tf_op jit(solution)/shard_map/send/pallas_call | solution.py:333
  2.2 20.3 %all_to_all.10.got_ref = bf16[32,13,4,128]{3,2,1,0:T(4,128)(2,1)S(1)} all-to-all(bf16[32,13,4,128]{3,2,1,0:T(4,128)(2,1)S(1)} %get-tuple-element.9), channel_id=1, replica_groups={{29,31,28,30,17,19,16,18,13,15,12,14,9,11,8,10,21,23,20,22,25,27,24,26,..., dimensions={0} | all-to-all | bytes 851968 | tf_op jit(solution)/shard_map/all_to_all | solution.py:28
  22.5 2.0 %receive.1 = (f32[16,24,384]{2,1,0:T(8,128)}, f32[16,24,384]{2,1,0:T(8,128)}, f32[32,1,128]{2,1,0:T(1,128)S(1)}) custom-call(bf16[32,13,4,128]{3,2,1,0:T(4,128)(2,1)S(1)} %all_to_all.10.got_ref, f32[16,24,384]{2,1,0:T(8,128)S(1)} %get-tuple-element.10.right_ref, bf16[1328,256]{1,0:T(8,128)(2,1)S(1)} %get-tuple-element.11.table_ref), custom_call_target="tpu_custom_call" | custom-call | tf_op jit(solution)/shard_map/receive/pallas_call | solution.py:359
  24.5 9.6 %all_to_all.11.parts_ref = f32[32,1,128]{2,1,0:T(1,128)S(1)} all-to-all(f32[32,1,128]{2,1,0:T(1,128)S(1)} %get-tuple-element.14), channel_id=1, replica_groups={{29,31,28,30,17,19,16,18,13,15,12,14,9,11,8,10,21,23,20,22,25,27,24,26,..., dimensions={0} | all-to-all | bytes 32768 | tf_op jit(solution)/shard_map/all_to_all | solution.py:28
  34.1 0.6 %finish.1 = f32[1,1]{1,0:T(1,128)} custom-call(f32[32,1,128]{2,1,0:T(1,128)S(1)} %all_to_all.11.parts_ref), custom_call_target="tpu_custom_call" | custom-call | tf_op jit(solution)/shard_map/finish/pallas_call | solution.py:380

commit v7 on v6

--- a/solution.py
+++ b/solution.py
@@ -213,7 +213,7 @@
 
 
 def receive_kernel(
-    order, cx, cy, got_ref, right_ref, table_ref, dec_hbm, res_hbm, sum_ref,
+    late, order, cx, cy, got_ref, right_ref, table_ref, dec_hbm, res_hbm, late_ref, sum_ref,
     high_ref, low_ref, edge_ref, dec_ref, res_ref, sems,
 ):
     peers = got_ref.shape[0]
@@ -287,12 +287,15 @@
         beside = beside + jnp.where(lane == 0, 0.0, pltpu.roll(here, 1, 1))
         beside = beside + jnp.where(lane == depth - 1, 0.0, pltpu.roll(here, depth - 1, 1))
         left = right_ref[x] - (6.0 * here - beside)
-        res_ref[x] = left
+        if x < late:
+            res_ref[x] = left
+        else:
+            late_ref[x - late] = left
         square = left * left
         for r in range(0, cy, 8):
             for c in range(0, depth, LANES):
                 total = total + square[r : r + 8, c : c + LANES]
-        if x % 4 == 3:
+        if x % 4 == 3 and x < late:
             part = pl.ds(x - 3, 4)
             store(res_ref.at[part], res_hbm.at[part])
         return total
@@ -311,10 +314,17 @@
         copy.wait()
 
 
-def finish_kernel(cells, parts_ref, rms_ref):
+def finish_kernel(cells, late, parts_ref, late_ref, res_in, rms_hbm, res_hbm, rms_ref, sems):
+    part = pl.ds(late, late_ref.shape[0])
+    stores = [pltpu.make_async_copy(late_ref, res_hbm.at[part], sems.at[0])]
+    stores += [pltpu.make_async_copy(rms_ref, rms_hbm, sems.at[1])]
+    stores[0].start()
     total = jnp.sum(parts_ref[...].reshape(-1, LANES), axis=0, keepdims=True)
     total = jnp.sum(total, axis=1, keepdims=True)
     rms_ref[...] = jnp.sqrt(total / cells + 1e-6)
+    stores[1].start()
+    for copy in stores:
+        copy.wait()
 
 
 def shards(count_x, count_y, coefficients, exponents, right_side):
@@ -356,35 +366,40 @@
         tables,
     )
     got = exchange(messages, order)
-    decoded, residual, parts = pl.pallas_call(
-        functools.partial(receive_kernel, order, cx, cy),
+    field = jax.ShapeDtypeStruct((cx, cy, depth), jnp.float32)
+    late = cx - cx // 4
+    decoded, residual, rest, parts = pl.pallas_call(
+        functools.partial(receive_kernel, late, order, cx, cy),
         out_shape=(
-            jax.ShapeDtypeStruct((cx, cy, depth), jnp.float32),
-            jax.ShapeDtypeStruct((cx, cy, depth), jnp.float32),
+            field,
+            field,
+            pltpu.VMEM((cx - late, cy, depth), jnp.float32),
             pltpu.VMEM((peers, 1, LANES), jnp.float32),
         ),
         in_specs=[vmem] * 3,
-        out_specs=(hbm, hbm, vmem),
+        out_specs=(hbm, hbm, vmem, vmem),
         scratch_shapes=[
             pltpu.VMEM((depth, 5 * LANES), jnp.bfloat16),
             pltpu.VMEM((depth, 5 * LANES), jnp.bfloat16),
             pltpu.VMEM((2 * cx + 2 * cy, depth), jnp.float32),
             pltpu.VMEM((cx, cy, depth), jnp.float32),
-            pltpu.VMEM((cx, cy, depth), jnp.float32),
-            pltpu.SemaphoreType.DMA((2 + cx // 4,)),
+            pltpu.VMEM((late, cy, depth), jnp.float32),
+            pltpu.SemaphoreType.DMA((2 + late // 4,)),
         ],
         compiler_params=pltpu.CompilerParams(vmem_limit_bytes=(12 << 20) * peers // 32),
         name="receive",
     )(got, right_side, tables)
     parts = exchange(parts, order)
-    rms = pl.pallas_call(
-        functools.partial(finish_kernel, patch * depth * peers),
-        out_shape=jax.ShapeDtypeStruct((1, 1), jnp.float32),
-        in_specs=[vmem],
-        out_specs=vmem,
+    rms, residual = pl.pallas_call(
+        functools.partial(finish_kernel, patch * depth * peers, late),
+        out_shape=(jax.ShapeDtypeStruct((1, 1), jnp.float32), field),
+        in_specs=[vmem, vmem, hbm],
+        out_specs=(hbm, hbm),
+        input_output_aliases={2: 1},
+        scratch_shapes=[pltpu.VMEM((1, 1), jnp.float32), pltpu.SemaphoreType.DMA((2,))],
         compiler_params=pltpu.CompilerParams(vmem_limit_bytes=1 << 20),
         name="finish",
-    )(parts)
+    )(parts, rest, residual)
     return (decoded, residual, rms.reshape(()))
 
 

time: 34.9 us -> 34.9 us (level)
  no operation moved by 1% of the time
where the time goes in v7:
time: 34.9 us; the launch traced here: 34.7 us
  blocking collectives  29.8 us (85%)
  Pallas kernels  4.2 us (12%)
  between operations  0.65 us (2%)
    all_to_all x2, blocking collectives, exchange(): lax.all_to_all(array, AXES, split_axis=0, concat_axis=0, tiled=True, axis...  29.8 us
    pallas_call x1, Pallas kernels, shards(): pl.pallas_call(functools.partial(receive_kernel, late, order, cx, cy), ou...  1.94 us
    pallas_call x1, Pallas kernels, shards(): pl.pallas_call(functools.partial(send_kernel, order, count_x, count_y, cx...  1.57 us

profile of v7, /device:TPU:0, one launch (start us, length us, event | category | flops | bytes accessed | tf_op | source)
XLA Modules:
  0.0 34.7 jit_solution(1797168135434310976)
XLA Ops:
  0.6 1.6 %send.1 = (bf16[32,13,4,128]{3,2,1,0:T(4,128)(2,1)S(1)}, f32[16,24,384]{2,1,0:T(8,128)S(1)}, bf16[1328,256]{1,0:T(8,128)(2,1)S(1)}) custom-call(bf16[12,12288]{1,0:T(8,128)(2,1)} %coef_hbm.1, s32[3,768]{1,0:T(4,128)} %exp_hbm.1, bf16[384,256]{1,0:T(8,128)(2,1)} %constant.5.clone.edge_hbm, f32[16,24,384]{2,1,0:T(8,128)} %right_hbm.1, ...), custom_call_target="tpu_custom_call" | custom-call | tf_op jit(solution)/shard_map/send/pallas_call | solution.py:343
  2.2 20.3 %all_to_all.10.got_ref = bf16[32,13,4,128]{3,2,1,0:T(4,128)(2,1)S(1)} all-to-all(bf16[32,13,4,128]{3,2,1,0:T(4,128)(2,1)S(1)} %get-tuple-element.12), channel_id=1, replica_groups={{29,31,28,30,17,19,16,18,13,15,12,14,9,11,8,10,21,23,20,22,25,27,24,26,..., dimensions={0} | all-to-all | bytes 851968 | tf_op jit(solution)/shard_map/all_to_all | solution.py:28
  22.5 1.9 %receive.1 = (f32[16,24,384]{2,1,0:T(8,128)}, f32[16,24,384]{2,1,0:T(8,128)}, f32[4,24,384]{2,1,0:T(8,128)S(1)}, f32[32,1,128]{2,1,0:T(1,128)S(1)}) custom-call(bf16[32,13,4,128]{3,2,1,0:T(4,128)(2,1)S(1)} %all_to_all.10.got_ref, f32[16,24,384]{2,1,0:T(8,128)S(1)} %get-tuple-element.13.right_ref, bf16[1328,256]{1,0:T(8,128)(2,1)S(1)} %get-tuple-element.14.table_ref), custom_call_target="tpu_custom_call" | custom-call | tf_op jit(solution)/shard_map/receive/pallas_call | solution.py:371
  24.4 9.6 %all_to_all.11.parts_ref = f32[32,1,128]{2,1,0:T(1,128)S(1)} all-to-all(f32[32,1,128]{2,1,0:T(1,128)S(1)} %get-tuple-element.16), channel_id=1, replica_groups={{29,31,28,30,17,19,16,18,13,15,12,14,9,11,8,10,21,23,20,22,25,27,24,26,..., dimensions={0} | all-to-all | bytes 32768 | tf_op jit(solution)/shard_map/all_to_all | solution.py:28
  34.0 0.7 %finish.1 = (f32[1,1]{1,0:T(1,128)}, f32[16,24,384]{2,1,0:T(8,128)}) custom-call(f32[32,1,128]{2,1,0:T(1,128)S(1)} %all_to_all.11.parts_ref, f32[4,24,384]{2,1,0:T(8,128)S(1)} %get-tuple-element.17.late_ref, f32[16,24,384]{2,1,0:T(8,128)} %get-tuple-element.18.res_in), custom_call_target="tpu_custom_call", output_to_operand_aliasing={{1}: (2, {})} | custom-call | tf_op jit(solution)/shard_map/finish/pallas_call | solution.py:393

commit v8 on v6

--- a/solution.py
+++ b/solution.py
@@ -250,12 +250,15 @@
                     value = jnp.where(in_block, value, 0.0)
                 high, low = split(value)
                 high_ref[at : at + count, t * LANES : (t + 1) * LANES] = high
-                low_ref[at : at + count, t * LANES : (t + 1) * LANES] = low
+                if t < 4:
+                    low_ref[at : at + count, t * LANES : (t + 1) * LANES] = low
 
     def across(tables, refs, start):
         return lax.dot_general(
             jnp.concatenate(tables, axis=1),
-            jnp.concatenate([ref[:, start : start + 2 * LANES] for ref in refs], axis=1),
+            jnp.concatenate(
+                [ref[:, start : start + t.shape[1]] for t, ref in zip(tables, refs)], axis=1
+            ),
             (((1,), (1,)), ((), ())),
             preferred_element_type=jnp.float32,
         )
@@ -299,7 +302,7 @@
 
     total = jnp.zeros((8, LANES), jnp.float32)
     decode(0, 0)
-    edge_ref[...] = across([table[6], table[6]], [high_ref, low_ref], patch)
+    edge_ref[...] = across([table[6], table[6][:, :LANES]], [high_ref, low_ref], patch)
     for x in range(cx // 2 - 1):
         total = finish(x, total)
     decode(1, patch - 2 * LANES)
@@ -367,7 +370,7 @@
         out_specs=(hbm, hbm, vmem),
         scratch_shapes=[
             pltpu.VMEM((depth, 5 * LANES), jnp.bfloat16),
-            pltpu.VMEM((depth, 5 * LANES), jnp.bfloat16),
+            pltpu.VMEM((depth, 4 * LANES), jnp.bfloat16),
             pltpu.VMEM((2 * cx + 2 * cy, depth), jnp.float32),
             pltpu.VMEM((cx, cy, depth), jnp.float32),
             pltpu.VMEM((cx, cy, depth), jnp.float32),

time: 34.9 us -> 35 us (level)
  no operation moved by 1% of the time
where the time goes in v8:
time: 35 us; the launch traced here: 34.8 us
  blocking collectives  29.8 us (85%)
  Pallas kernels  4.28 us (12%)
  between operations  0.65 us (2%)
    all_to_all x2, blocking collectives, exchange(): lax.all_to_all(array, AXES, split_axis=0, concat_axis=0, tiled=True, axis...  29.8 us
    pallas_call x1, Pallas kernels, shards(): pl.pallas_call(functools.partial(receive_kernel, order, cx, cy), out_shap...  2.09 us
    pallas_call x1, Pallas kernels, shards(): pl.pallas_call(functools.partial(send_kernel, order, count_x, count_y, cx...  1.57 us

profile of v8, /device:TPU:0, one launch (start us, length us, event | category | flops | bytes accessed | tf_op | source)
XLA Modules:
  0.0 34.8 jit_solution(4192958511634852300)
XLA Ops:
  0.6 1.6 %send.1 = (bf16[32,13,4,128]{3,2,1,0:T(4,128)(2,1)S(1)}, f32[16,24,384]{2,1,0:T(8,128)S(1)}, bf16[1328,256]{1,0:T(8,128)(2,1)S(1)}) custom-call(bf16[12,12288]{1,0:T(8,128)(2,1)} %coef_hbm.1, s32[3,768]{1,0:T(4,128)} %exp_hbm.1, bf16[384,256]{1,0:T(8,128)(2,1)} %constant.5.clone.edge_hbm, f32[16,24,384]{2,1,0:T(8,128)} %right_hbm.1, ...), custom_call_target="tpu_custom_call" | custom-call | tf_op jit(solution)/shard_map/send/pallas_call | solution.py:336
  2.2 20.3 %all_to_all.10.got_ref = bf16[32,13,4,128]{3,2,1,0:T(4,128)(2,1)S(1)} all-to-all(bf16[32,13,4,128]{3,2,1,0:T(4,128)(2,1)S(1)} %get-tuple-element.9), channel_id=1, replica_groups={{29,31,28,30,17,19,16,18,13,15,12,14,9,11,8,10,21,23,20,22,25,27,24,26,..., dimensions={0} | all-to-all | bytes 851968 | tf_op jit(solution)/shard_map/all_to_all | solution.py:28
  22.5 2.1 %receive.1 = (f32[16,24,384]{2,1,0:T(8,128)}, f32[16,24,384]{2,1,0:T(8,128)}, f32[32,1,128]{2,1,0:T(1,128)S(1)}) custom-call(bf16[32,13,4,128]{3,2,1,0:T(4,128)(2,1)S(1)} %all_to_all.10.got_ref, f32[16,24,384]{2,1,0:T(8,128)S(1)} %get-tuple-element.10.right_ref, bf16[1328,256]{1,0:T(8,128)(2,1)S(1)} %get-tuple-element.11.table_ref), custom_call_target="tpu_custom_call" | custom-call | tf_op jit(solution)/shard_map/receive/pallas_call | solution.py:362
  24.6 9.6 %all_to_all.11.parts_ref = f32[32,1,128]{2,1,0:T(1,128)S(1)} all-to-all(f32[32,1,128]{2,1,0:T(1,128)S(1)} %get-tuple-element.14), channel_id=1, replica_groups={{29,31,28,30,17,19,16,18,13,15,12,14,9,11,8,10,21,23,20,22,25,27,24,26,..., dimensions={0} | all-to-all | bytes 32768 | tf_op jit(solution)/shard_map/all_to_all | solution.py:28
  34.1 0.6 %finish.1 = f32[1,1]{1,0:T(1,128)} custom-call(f32[32,1,128]{2,1,0:T(1,128)S(1)} %all_to_all.11.parts_ref), custom_call_target="tpu_custom_call" | custom-call | tf_op jit(solution)/shard_map/finish/pallas_call | solution.py:383
